TPU v7x, 32 devices: a whole 2x2x4 slice. The times are simulated.
32 devices in a mesh: vocab: 32 (over z, y, x, core).
Axes of the slice: x: 2, y: 2, z: 4, core: 2. Of those that a mesh axis runs over, the one named last changes fastest.
Arguments:
- hidden: bfloat16 [2, 256, 3584], P(None, 'vocab'), may hold values from -256 to 256
- head_weight: bfloat16 [3584, 24576], P(None, 'vocab'), may hold values from -1 to 1
- teacher: bfloat16 [2, 256, 24576], P(None, None, 'vocab'), may hold values from 0 to 1
Outputs:
- token_loss: float32 [2, 256], P(None, 'vocab')
- hidden_grad: bfloat16 [2, 256, 3584], P(None, 'vocab')
- head_grad: bfloat16 [3584, 24576], P(None, 'vocab')
All inputs are finite; a program needn't handle non-finite values.
Results may differ from a plain program's by a relative error of at most 0.012.
Values may be sent and summed in bfloat16 or wider, within the bound.
No kernel may reach another device: no remote copies, remote signals or barrier semaphores. Data moves between devices by JAX's collectives and lax.ppermute only.
A program may use at most 128 MiB of HBM per device.

v0:
```python
import functools

import jax
import jax.numpy as jnp
from jax import lax
from jax.experimental import pallas as pl
from jax.experimental.pallas import tpu as pltpu
from jax.sharding import PartitionSpec as P

AXIS = "vocab"
ROW_TILE = 8
STATS_RADIX_BITS = 2
VMEM_BYTES = 12 << 20


def stage_orders(size, groups):
    bits = list(range(size.bit_length() - 2, 0, -1))
    low, high = [], []
    for start in range(0, len(bits), 2):
        pair = bits[start : start + 2]
        low += pair if start == 0 else pair[::-1]
        high += pair[::-1] if start == 0 else pair
    return [[low, high] for _ in range(groups)]


def masks_of(order):
    masks = [0]
    for bit in order:
        masks += [mask | (1 << bit) for mask in masks]
    return tuple(masks)


def owner_of(me, masks, block):
    half = len(masks[0])
    core = lax.rem(me, 2)
    if block < half:
        return me ^ jnp.where(core == 0, masks[0][block], masks[1][block])
    block -= half
    return me ^ 1 ^ jnp.where(core == 0, masks[1][block], masks[0][block])


def swap(value, order_pair, stage, size):
    pairs = [(i, i ^ (1 << order_pair[i & 1][stage])) for i in range(size)]
    return lax.ppermute(value, AXIS, pairs)


def swap_core(value, size):
    return lax.ppermute(value, AXIS, [(i, i ^ 1) for i in range(size)])


def stats_kernel(masks, me_ref, teacher_ref, *refs):
    me = me_ref[0]
    groups = teacher_ref.shape[0]
    own_refs, pair_refs, out_ref = refs[:groups], refs[groups : 2 * groups], refs[2 * groups]
    half = len(masks[0][0])
    size = 2 * half
    lane = lax.broadcasted_iota(jnp.int32, (ROW_TILE, groups * size), 1)
    norm_all = jnp.zeros((ROW_TILE, groups * size), jnp.float32)
    mass_all = norm_all
    cross_all = norm_all
    for block in range(size):
        source = own_refs if block < half else pair_refs
        for group in range(groups):
            owner = owner_of(me, masks[group], block)
            start = pl.multiple_of(owner * ROW_TILE, ROW_TILE)
            logits = source[group][pl.ds((block % half) * ROW_TILE, ROW_TILE), :]
            target = teacher_ref[group, pl.ds(start, ROW_TILE), :].astype(jnp.float32)
            peak = jnp.max(logits, axis=1, keepdims=True)
            total = jnp.sum(jnp.exp(logits - peak), axis=1, keepdims=True)
            mass = jnp.sum(target, axis=1, keepdims=True)
            cross = jnp.sum(target * logits, axis=1, keepdims=True)
            here = lane == group * size + owner
            norm_all = jnp.where(here, peak + jnp.log(total), norm_all)
            mass_all = jnp.where(here, mass, mass_all)
            cross_all = jnp.where(here, cross, cross_all)
    out_ref[0] = norm_all
    out_ref[1] = mass_all
    out_ref[2] = cross_all


def grad_kernel(masks, me_ref, stats_ref, teacher_ref, *refs):
    me = me_ref[0]
    groups = teacher_ref.shape[0]
    own_refs, pair_refs = refs[:groups], refs[groups : 2 * groups]
    loss_ref, own_grad_ref, pair_grad_ref = refs[2 * groups :]
    half = len(masks[0][0])
    size = 2 * half
    log_norm, mass, cross = stats_ref[0], stats_ref[1], stats_ref[2]
    loss = mass * log_norm - cross
    lane = lax.broadcasted_iota(jnp.int32, mass.shape, 1)
    square = (ROW_TILE, ROW_TILE)
    diagonal = lax.broadcasted_iota(jnp.int32, square, 0) == lax.broadcasted_iota(jnp.int32, square, 1)
    for group in range(groups):
        column = jnp.sum(jnp.where(lane == group * size + me, loss, 0.0), axis=1, keepdims=True)
        loss_ref[pl.ds(group, 1), :] = jnp.sum(jnp.where(diagonal, column, 0.0), axis=0, keepdims=True)
    for block in range(size):
        source = own_refs if block < half else pair_refs
        result = own_grad_ref if block < half else pair_grad_ref
        for group in range(groups):
            owner = owner_of(me, masks[group], block)
            start = pl.multiple_of(owner * ROW_TILE, ROW_TILE)
            logits = source[group][pl.ds((block % half) * ROW_TILE, ROW_TILE), :]
            here = lane == group * size + owner
            norm_rows = jnp.sum(jnp.where(here, log_norm, 0.0), axis=1, keepdims=True)
            mass_rows = jnp.sum(jnp.where(here, mass, 0.0), axis=1, keepdims=True)
            target = teacher_ref[group, pl.ds(start, ROW_TILE), :].astype(jnp.float32)
            grad = mass_rows * jnp.exp(logits - norm_rows) - target
            result[pl.ds((group * half + block % half) * ROW_TILE, ROW_TILE), :] = grad.astype(jnp.bfloat16)


def vmem(count):
    return [pl.BlockSpec(memory_space=pltpu.VMEM)] * count


def call_stats(me, own, pair, teacher, masks):
    groups, size = teacher.shape[0], 2 * len(masks[0][0])
    return pl.pallas_call(
        functools.partial(stats_kernel, masks),
        out_shape=jax.ShapeDtypeStruct((3, ROW_TILE, groups * size), jnp.float32),
        in_specs=[pl.BlockSpec(memory_space=pltpu.SMEM)] + vmem(2 * groups + 1),
        out_specs=vmem(1)[0],
        cost_estimate=pl.CostEstimate(flops=2_000_000, bytes_accessed=2_400_000, transcendentals=400_000),
        compiler_params=pltpu.CompilerParams(vmem_limit_bytes=VMEM_BYTES),
        name="stats",
    )(me, teacher, *own, *pair)


def call_grad(me, stats, own, pair, teacher, masks):
    groups = len(own)
    grad = jax.ShapeDtypeStruct((groups * own[0].shape[0], own[0].shape[1]), jnp.bfloat16)
    return pl.pallas_call(
        functools.partial(grad_kernel, masks),
        out_shape=[jax.ShapeDtypeStruct((groups, ROW_TILE), jnp.float32), grad, grad],
        in_specs=[pl.BlockSpec(memory_space=pltpu.SMEM)] + vmem(2 * groups + 2),
        out_specs=vmem(3),
        cost_estimate=pl.CostEstimate(flops=2_000_000, bytes_accessed=3_200_000, transcendentals=400_000),
        compiler_params=pltpu.CompilerParams(vmem_limit_bytes=VMEM_BYTES),
        name="grad",
    )(me, stats, teacher, *own, *pair)


def joined(own, pair, size):
    parts = [jnp.stack(part).reshape(len(part), size // 2, -1, part[0].shape[-1]) for part in (own, pair)]
    return jnp.concatenate(parts, axis=1)


def taken(values, owners):
    return jnp.stack([jnp.take(value, owner, axis=0) for value, owner in zip(values, owners)])


def plain_stats(owners, own, pair, teacher):
    logits = joined(own, pair, teacher.shape[1])
    target = taken(teacher, owners).astype(jnp.float32)
    peak = jnp.max(logits, axis=-1)
    norm = peak + jnp.log(jnp.sum(jnp.exp(logits - peak[..., None]), axis=-1))
    stats = jnp.stack([norm, jnp.sum(target, axis=-1), jnp.sum(target * logits, axis=-1)])
    back = [jnp.zeros_like(stats[:, 0]).at[:, owner].set(stats[:, group]) for group, owner in enumerate(owners)]
    return jnp.stack(back, axis=1)


def plain_grad(me, owners, stats, own, pair, teacher):
    size, _, width = teacher.shape[1:]
    log_norm, mass, cross = stats
    loss = lax.dynamic_index_in_dim(mass * log_norm - cross, me, axis=1, keepdims=False)
    shifted = joined(own, pair, size) - taken(log_norm, owners)[..., None]
    grad = taken(mass, owners)[..., None] * jnp.exp(shifted) - taken(teacher, owners).astype(jnp.float32)
    grad = grad.astype(jnp.bfloat16)
    own_grad, pair_grad = grad[:, : size // 2], grad[:, size // 2 :]
    return loss, own_grad.reshape(-1, width), pair_grad.reshape(-1, width)


def merge_stats(left, right):
    plane = lax.broadcasted_iota(jnp.int32, left.shape, 0)
    high, low = jnp.maximum(left, right), jnp.minimum(left, right)
    return jnp.where(plane == 0, high + jnp.log1p(jnp.exp(low - high)), left + right)


def exchange_stats(stats, size):
    stats = merge_stats(stats, swap_core(stats, size))
    bits = list(range(1, size.bit_length() - 1))
    while bits:
        step, bits = bits[:STATS_RADIX_BITS], bits[STATS_RADIX_BITS:]
        got = [lax.ppermute(stats, AXIS, [(i, i ^ mask) for i in range(size)]) for mask in masks_of(step)[1:]]
        for value in got:
            stats = merge_stats(stats, value)
    return stats


def matmul(left, right, contract):
    return lax.dot_general(left, right, (contract, ((), ())), preferred_element_type=jnp.float32)


def add_round(left, right):
    return (left.astype(jnp.float32) + right.astype(jnp.float32)).astype(jnp.bfloat16)


def shards(hidden, head_weight, teacher):
    groups, row_count, _ = hidden.shape
    size = lax.axis_size(AXIS)
    me = lax.axis_index(AXIS)
    walks = stage_orders(size, groups)
    masks = [[masks_of(order) for order in walk] for walk in walks]
    stages = len(walks[0][0])
    width = head_weight.shape[1]

    held = [hidden[group] for group in range(groups)]
    for stage in range(stages):
        for group in range(groups):
            rows = lax.optimization_barrier(held[group])
            got = swap(rows, walks[group], stage, size)
            held[group] = jnp.concatenate([rows, got])
    held = [lax.optimization_barrier(rows) for rows in held]
    other, own, pair = [], [], []
    for group in range(groups):
        other.append(swap_core(held[group], size))
        own.append(matmul(held[group], head_weight, ((1,), (0,))))
        pair.append(matmul(other[group], head_weight, ((1,), (0,))))

    if row_count == ROW_TILE:
        stats = exchange_stats(call_stats(me.reshape(1), own, pair, teacher, masks), size)
        loss, own_grad, pair_grad = call_grad(me.reshape(1), stats, own, pair, teacher, masks)
    else:
        owners = [jnp.stack([owner_of(me, masks[group], block) for block in range(size)]) for group in range(groups)]
        blocks = teacher.reshape(groups, size, row_count, width)
        stats = exchange_stats(plain_stats(owners, own, pair, blocks), size)
        loss, own_grad, pair_grad = plain_grad(me, owners, stats, own, pair, blocks)

    sent = matmul(pair_grad, head_weight, ((1,), (1,))).astype(jnp.bfloat16)
    sent, mine = lax.optimization_barrier((sent, own_grad))
    kept = matmul(mine, head_weight, ((1,), (1,)))
    half = kept.shape[0] // groups
    kept = lax.optimization_barrier([kept[group * half : (group + 1) * half] for group in range(groups)])
    totals = []
    for group in range(groups):
        rows = slice(group * half, (group + 1) * half)
        got = swap_core(sent[rows], size)
        totals.append(add_round(kept[group], got))

    row_blocks = jnp.concatenate([*held, *other])
    grad_blocks = jnp.concatenate([own_grad, pair_grad])
    weight_grad = matmul(row_blocks, grad_blocks, ((0,), (0,)))

    for stage in reversed(range(stages)):
        rows = totals[0].shape[0] // 2
        for group in range(groups):
            got = swap(totals[group][rows:], walks[group], stage, size)
            totals[group] = add_round(totals[group][:rows], got)
    return (loss, jnp.stack(totals), weight_grad.astype(jnp.bfloat16))


def solution(mesh):
    in_specs = (P(None, AXIS, None), P(None, AXIS), P(None, None, AXIS))
    out_specs = (P(None, AXIS), P(None, AXIS, None), P(None, AXIS))

    return jax.shard_map(shards, mesh=mesh, in_specs=in_specs, out_specs=out_specs, check_vma=False)
```

profile of v0, /device:TPU:0, one launch (start us, length us, event | category | flops | bytes accessed | tf_op | source)
XLA Modules:
  0.0 101.5 jit_solution(8678088169760380713)
XLA Ops:
  1.5 4.1 %collective-permute-start = (bf16[8,3584]{1,0:T(8,128)(2,1)S(1)}, bf16[8,3584]{1,0:T(8,128)(2,1)S(1)}, u32[]{:S(2)}, u32[]{:S(2)}) collective-permute-start(bf16[8,3584]{1,0:T(8,128)(2,1)S(1)} %get-tuple-element.22), channel_id=1, source_target_pairs={{0,16},{1,9},{2,18},{3,11},{4,20},{5,13},{6,22},{7,15},{8,24},{9,1... | collective-permute-start | bytes 172040 | tf_op jit(solution)/shard_map/ppermute | solution.py:44
  5.7 2.2 %collective-permute-done = bf16[8,3584]{1,0:T(8,128)(2,1)S(1)} collective-permute-done((bf16[8,3584]{1,0:T(8,128)(2,1)S(1)}, bf16[8,3584]{1,0:T(8,128)(2,1)S(1)}, u32[]{:S(2)}, u32[]{:S(2)}) %collective-permute-start) | collective-permute-done | bytes 57376 | tf_op jit(solution)/shard_map/ppermute | solution.py:44
  7.9 2.2 %collective-permute-start.1 = (bf16[16,3584]{1,0:T(8,128)(2,1)S(1)}, bf16[16,3584]{1,0:T(8,128)(2,1)S(1)}, u32[]{:S(2)}, u32[]{:S(2)}) collective-permute-start(bf16[16,3584]{1,0:T(8,128)(2,1)S(1)} %pad_maximum_fusion.6), channel_id=1, source_target_pairs={{0,8},{1,17},{2,10},{3,19},{4,12},{5,21},{6,14},{7,23},{8,0},{9,25... | collective-permute-start | bytes 344072 | tf_op jit(solution)/shard_map/ppermute | solution.py:44
  10.1 4.3 %collective-permute-done.4 = bf16[8,3584]{1,0:T(8,128)(2,1)S(1)} collective-permute-done((bf16[8,3584]{1,0:T(8,128)(2,1)S(1)}, bf16[8,3584]{1,0:T(8,128)(2,1)S(1)}, u32[]{:S(2)}, u32[]{:S(2)}) %collective-permute-start.4) | collective-permute-done | bytes 57376 | tf_op jit(solution)/shard_map/ppermute | solution.py:44
  14.5 1.6 %collective-permute-start.2 = (bf16[32,3584]{1,0:T(8,128)(2,1)S(1)}, bf16[32,3584]{1,0:T(8,128)(2,1)S(1)}, u32[]{:S(2)}, u32[]{:S(2)}) collective-permute-start(bf16[32,3584]{1,0:T(8,128)(2,1)S(1)} %pad_maximum_fusion.4), channel_id=1, source_target_pairs={{0,2},{1,5},{2,0},{3,7},{4,6},{5,1},{6,4},{7,3},{8,10},{9,13},{10,... | collective-permute-start | bytes 688136 | tf_op jit(solution)/shard_map/ppermute | solution.py:44
  16.1 3.2 %collective-permute-done.5 = bf16[16,3584]{1,0:T(8,128)(2,1)S(1)} collective-permute-done((bf16[16,3584]{1,0:T(8,128)(2,1)S(1)}, bf16[16,3584]{1,0:T(8,128)(2,1)S(1)}, u32[]{:S(2)}, u32[]{:S(2)}) %collective-permute-start.5) | collective-permute-done | bytes 114720 | tf_op jit(solution)/shard_map/ppermute | solution.py:44
  19.3 1.6 %collective-permute-start.6 = (bf16[32,3584]{1,0:T(8,128)(2,1)S(1)}, bf16[32,3584]{1,0:T(8,128)(2,1)S(1)}, u32[]{:S(2)}, u32[]{:S(2)}) collective-permute-start(bf16[32,3584]{1,0:T(8,128)(2,1)S(1)} %pad_maximum_fusion.5), channel_id=1, source_target_pairs={{0,2},{1,5},{2,0},{3,7},{4,6},{5,1},{6,4},{7,3},{8,10},{9,13},{10,... | collective-permute-start | bytes 688136 | tf_op jit(solution)/shard_map/ppermute | solution.py:44
  20.9 1.6 %collective-permute-start.3 = (bf16[64,3584]{1,0:T(8,128)(2,1)S(1)}, bf16[64,3584]{1,0:T(8,128)(2,1)S(1)}, u32[]{:S(2)}, u32[]{:S(2)}) collective-permute-start(bf16[64,3584]{1,0:T(8,128)(2,1)S(1)} %pad_maximum_fusion.2), channel_id=1, source_target_pairs={{0,4},{1,3},{2,6},{3,1},{4,0},{5,7},{6,2},{7,5},{8,12},{9,11},{10,... | collective-permute-start | bytes 1376264 | tf_op jit(solution)/shard_map/ppermute | solution.py:44
  22.4 5.4 %collective-permute-done.6 = bf16[32,3584]{1,0:T(8,128)(2,1)S(1)} collective-permute-done((bf16[32,3584]{1,0:T(8,128)(2,1)S(1)}, bf16[32,3584]{1,0:T(8,128)(2,1)S(1)}, u32[]{:S(2)}, u32[]{:S(2)}) %collective-permute-start.6) | collective-permute-done | bytes 229408 | tf_op jit(solution)/shard_map/ppermute | solution.py:44
  27.8 1.6 %collective-permute-start.7 = (bf16[64,3584]{1,0:T(8,128)(2,1)S(1)}, bf16[64,3584]{1,0:T(8,128)(2,1)S(1)}, u32[]{:S(2)}, u32[]{:S(2)}) collective-permute-start(bf16[64,3584]{1,0:T(8,128)(2,1)S(1)} %pad_maximum_fusion.3), channel_id=1, source_target_pairs={{0,4},{1,3},{2,6},{3,1},{4,0},{5,7},{6,2},{7,5},{8,12},{9,11},{10,... | collective-permute-start | bytes 1376264 | tf_op jit(solution)/shard_map/ppermute | solution.py:44
  29.7 6.7 %collective-permute-done.7 = bf16[64,3584]{1,0:T(8,128)(2,1)S(1)} collective-permute-done((bf16[64,3584]{1,0:T(8,128)(2,1)S(1)}, bf16[64,3584]{1,0:T(8,128)(2,1)S(1)}, u32[]{:S(2)}, u32[]{:S(2)}) %collective-permute-start.7) | collective-permute-done | bytes 458784 | tf_op jit(solution)/shard_map/ppermute | solution.py:44
  42.5 2.5 %collective-permute-start.13 = (f32[3,8,64]{2,1,0:T(8,128)S(1)}, f32[3,8,64]{2,1,0:T(8,128)S(1)}, u32[]{:S(2)}, u32[]{:S(2)}) collective-permute-start(f32[3,8,64]{2,1,0:T(8,128)S(1)} %add_select_fusion.2), channel_id=1, source_target_pairs={{0,6},{1,7},{2,4},{3,5},{4,2},{5,3},{6,0},{7,1},{8,14},{9,15},{10,... | collective-permute-start | bytes 18440 | tf_op jit(solution)/shard_map/ppermute | solution.py:183
  49.3 3.6 %collective-permute-start.16 = (f32[3,8,64]{2,1,0:T(8,128)S(1)}, f32[3,8,64]{2,1,0:T(8,128)S(1)}, u32[]{:S(2)}, u32[]{:S(2)}) collective-permute-start(f32[3,8,64]{2,1,0:T(8,128)S(1)} %add_select_fusion.1), channel_id=1, source_target_pairs={{0,24},{1,25},{2,26},{3,27},{4,28},{5,29},{6,30},{7,31},{8,16},{9,... | collective-permute-start | bytes 18440 | tf_op jit(solution)/shard_map/ppermute | solution.py:183
  54.9 2.5 %collective-permute-done.15 = f32[3,8,64]{2,1,0:T(8,128)S(1)} collective-permute-done((f32[3,8,64]{2,1,0:T(8,128)S(1)}, f32[3,8,64]{2,1,0:T(8,128)S(1)}, u32[]{:S(2)}, u32[]{:S(2)}) %collective-permute-start.15) | collective-permute-done | bytes 6176 | tf_op jit(solution)/shard_map/ppermute | solution.py:183
  58.6 1.6 %convolution_convert_fusion.1 = bf16[256,3584]{1,0:T(8,128)(2,1)S(1)} fusion(bf16[256,768]{1,0:T(8,128)(2,1)S(1)} %get-tuple-element.11, bf16[3584,768]{1,0:T(8,128)(2,1)S(1)} %copy-done.1), kind=kOutput, calls=%fused_computation.1 | convolution fusion | flops 1410203648 | bytes 7733248 | tf_op jit(solution)/shard_map/dot_general | solution.py:190
  60.2 1.6 %fusion.19 = f32[256,3584]{1,0:T(8,128)S(1)} fusion(bf16[256,768]{1,0:T(8,128)(2,1)S(1)} %get-tuple-element.13, bf16[3584,768]{1,0:T(8,128)(2,1)S(1)} %copy-done.1), kind=kOutput, calls=%fused_computation.46 | convolution fusion | flops 1409286144 | bytes 9568256 | tf_op jit(solution)/shard_map/dot_general | solution.py:190
  62.9 4.8 %convolution_convert_fusion = bf16[3584,768]{1,0:T(8,128)(2,1)} fusion(bf16[128,3584]{1,0:T(8,128)(2,1)S(1)} %collective-permute-done.9, bf16[128,3584]{1,0:T(8,128)(2,1)S(1)} %collective-permute-done.8, bf16[128,3584]{1,0:T(8,128)(2,1)S(1)} %pad_maximum_fusion.1, bf16[128,3584]{1,0:T(8,128)(2,1)S(1)} %pad_maximum_fusion, ...), kind=kOutput, calls=%fused_computation | convolution fusion | flops 2837577728 | bytes 9961472 | tf_op jit(solution)/shard_map/dot_general | solution.py:190
  67.9 1.6 %collective-permute-start.23 = (bf16[64,3584]{1,0:T(8,128)(2,1)S(1)}, bf16[64,3584]{1,0:T(8,128)(2,1)S(1)}, u32[]{:S(2)}, u32[]{:S(2)}) collective-permute-start(bf16[64,3584]{1,0:T(8,128)(2,1)S(1)} %slice.99), channel_id=1, source_target_pairs={{0,4},{1,3},{2,6},{3,1},{4,0},{5,7},{6,2},{7,5},{8,12},{9,11},{10,... | collective-permute-start | bytes 1376264 | tf_op jit(solution)/shard_map/ppermute | solution.py:44
  70.3 6.2 %collective-permute-done.23 = bf16[64,3584]{1,0:T(8,128)(2,1)S(1)} collective-permute-done((bf16[64,3584]{1,0:T(8,128)(2,1)S(1)}, bf16[64,3584]{1,0:T(8,128)(2,1)S(1)}, u32[]{:S(2)}, u32[]{:S(2)}) %collective-permute-start.23) | collective-permute-done | bytes 458784 | tf_op jit(solution)/shard_map/ppermute | solution.py:44
  77.2 6.6 %collective-permute-done.18 = bf16[64,3584]{1,0:T(8,128)(2,1)S(1)} collective-permute-done((bf16[64,3584]{1,0:T(8,128)(2,1)S(1)}, bf16[64,3584]{1,0:T(8,128)(2,1)S(1)}, u32[]{:S(2)}, u32[]{:S(2)}) %collective-permute-start.18) | collective-permute-done | bytes 458784 | tf_op jit(solution)/shard_map/ppermute | solution.py:44
  85.0 5.1 %collective-permute-done.19 = bf16[32,3584]{1,0:T(8,128)(2,1)S(1)} collective-permute-done((bf16[32,3584]{1,0:T(8,128)(2,1)S(1)}, bf16[32,3584]{1,0:T(8,128)(2,1)S(1)}, u32[]{:S(2)}, u32[]{:S(2)}) %collective-permute-start.19) | collective-permute-done | bytes 229408 | tf_op jit(solution)/shard_map/ppermute | solution.py:44
  92.6 2.8 %collective-permute-done.20 = bf16[16,3584]{1,0:T(8,128)(2,1)S(1)} collective-permute-done((bf16[16,3584]{1,0:T(8,128)(2,1)S(1)}, bf16[16,3584]{1,0:T(8,128)(2,1)S(1)}, u32[]{:S(2)}, u32[]{:S(2)}) %collective-permute-start.20) | collective-permute-done | bytes 114720 | tf_op jit(solution)/shard_map/ppermute | solution.py:44
  95.5 2.3 %collective-permute-start.21 = (bf16[8,3584]{1,0:T(8,128)(2,1)S(1)}, bf16[8,3584]{1,0:T(8,128)(2,1)S(1)}, u32[]{:S(2)}, u32[]{:S(2)}) collective-permute-start(bf16[8,3584]{1,0:T(8,128)(2,1)S(1)} %slice.97), channel_id=1, source_target_pairs={{0,16},{1,9},{2,18},{3,11},{4,20},{5,13},{6,22},{7,15},{8,24},{9,1... | collective-permute-start | bytes 172040 | tf_op jit(solution)/shard_map/ppermute | solution.py:44
  97.8 3.1 %collective-permute-done.21 = bf16[8,3584]{1,0:T(8,128)(2,1)S(1)} collective-permute-done((bf16[8,3584]{1,0:T(8,128)(2,1)S(1)}, bf16[8,3584]{1,0:T(8,128)(2,1)S(1)}, u32[]{:S(2)}, u32[]{:S(2)}) %collective-permute-start.21) | collective-permute-done | bytes 57376 | tf_op jit(solution)/shard_map/ppermute | solution.py:44
  (77 shorter events, 22.0 us)
Async XLA Ops:
  1.5 6.4 %collective-permute-start = (bf16[8,3584]{1,0:T(8,128)(2,1)S(1)}, bf16[8,3584]{1,0:T(8,128)(2,1)S(1)}, u32[]{:S(2)}, u32[]{:S(2)}) collective-permute-start(bf16[8,3584]{1,0:T(8,128)(2,1)S(1)} %get-tuple-element.22), channel_id=1, source_target_pairs={{0,16},{1,9},{2,18},{3,11},{4,20},{5,13},{6,22},{7,15},{8,24},{9,1... | collective-permute-start | bytes 172040 | tf_op jit(solution)/shard_map/ppermute | solution.py:44
  5.6 8.8 %collective-permute-start.4 = (bf16[8,3584]{1,0:T(8,128)(2,1)S(1)}, bf16[8,3584]{1,0:T(8,128)(2,1)S(1)}, u32[]{:S(2)}, u32[]{:S(2)}) collective-permute-start(bf16[8,3584]{1,0:T(8,128)(2,1)S(1)} %get-tuple-element.21), channel_id=1, source_target_pairs={{0,16},{1,9},{2,18},{3,11},{4,20},{5,13},{6,22},{7,15},{8,24},{9,1... | collective-permute-start | bytes 172040 | tf_op jit(solution)/shard_map/ppermute | solution.py:44
  7.9 6.6 %collective-permute-start.1 = (bf16[16,3584]{1,0:T(8,128)(2,1)S(1)}, bf16[16,3584]{1,0:T(8,128)(2,1)S(1)}, u32[]{:S(2)}, u32[]{:S(2)}) collective-permute-start(bf16[16,3584]{1,0:T(8,128)(2,1)S(1)} %pad_maximum_fusion.6), channel_id=1, source_target_pairs={{0,8},{1,17},{2,10},{3,19},{4,12},{5,21},{6,14},{7,23},{8,0},{9,25... | collective-permute-start | bytes 344072 | tf_op jit(solution)/shard_map/ppermute | solution.py:44
  14.4 4.9 %collective-permute-start.5 = (bf16[16,3584]{1,0:T(8,128)(2,1)S(1)}, bf16[16,3584]{1,0:T(8,128)(2,1)S(1)}, u32[]{:S(2)}, u32[]{:S(2)}) collective-permute-start(bf16[16,3584]{1,0:T(8,128)(2,1)S(1)} %pad_maximum_fusion.7), channel_id=1, source_target_pairs={{0,8},{1,17},{2,10},{3,19},{4,12},{5,21},{6,14},{7,23},{8,0},{9,25... | collective-permute-start | bytes 344072 | tf_op jit(solution)/shard_map/ppermute | solution.py:44
  14.5 6.3 %collective-permute-start.2 = (bf16[32,3584]{1,0:T(8,128)(2,1)S(1)}, bf16[32,3584]{1,0:T(8,128)(2,1)S(1)}, u32[]{:S(2)}, u32[]{:S(2)}) collective-permute-start(bf16[32,3584]{1,0:T(8,128)(2,1)S(1)} %pad_maximum_fusion.4), channel_id=1, source_target_pairs={{0,2},{1,5},{2,0},{3,7},{4,6},{5,1},{6,4},{7,3},{8,10},{9,13},{10,... | collective-permute-start | bytes 688136 | tf_op jit(solution)/shard_map/ppermute | solution.py:44
  19.3 8.5 %collective-permute-start.6 = (bf16[32,3584]{1,0:T(8,128)(2,1)S(1)}, bf16[32,3584]{1,0:T(8,128)(2,1)S(1)}, u32[]{:S(2)}, u32[]{:S(2)}) collective-permute-start(bf16[32,3584]{1,0:T(8,128)(2,1)S(1)} %pad_maximum_fusion.5), channel_id=1, source_target_pairs={{0,2},{1,5},{2,0},{3,7},{4,6},{5,1},{6,4},{7,3},{8,10},{9,13},{10,... | collective-permute-start | bytes 688136 | tf_op jit(solution)/shard_map/ppermute | solution.py:44
  20.9 8.6 %collective-permute-start.3 = (bf16[64,3584]{1,0:T(8,128)(2,1)S(1)}, bf16[64,3584]{1,0:T(8,128)(2,1)S(1)}, u32[]{:S(2)}, u32[]{:S(2)}) collective-permute-start(bf16[64,3584]{1,0:T(8,128)(2,1)S(1)} %pad_maximum_fusion.2), channel_id=1, source_target_pairs={{0,4},{1,3},{2,6},{3,1},{4,0},{5,7},{6,2},{7,5},{8,12},{9,11},{10,... | collective-permute-start | bytes 1376264 | tf_op jit(solution)/shard_map/ppermute | solution.py:44
  27.8 8.5 %collective-permute-start.7 = (bf16[64,3584]{1,0:T(8,128)(2,1)S(1)}, bf16[64,3584]{1,0:T(8,128)(2,1)S(1)}, u32[]{:S(2)}, u32[]{:S(2)}) collective-permute-start(bf16[64,3584]{1,0:T(8,128)(2,1)S(1)} %pad_maximum_fusion.3), channel_id=1, source_target_pairs={{0,4},{1,3},{2,6},{3,1},{4,0},{5,7},{6,2},{7,5},{8,12},{9,11},{10,... | collective-permute-start | bytes 1376264 | tf_op jit(solution)/shard_map/ppermute | solution.py:44
  29.5 8.8 %collective-permute-start.8 = (bf16[128,3584]{1,0:T(8,128)(2,1)S(1)}, bf16[128,3584]{1,0:T(8,128)(2,1)S(1)}, u32[]{:S(2)}, u32[]{:S(2)}) collective-permute-start(bf16[128,3584]{1,0:T(8,128)(2,1)S(1)} %pad_maximum_fusion), channel_id=1, source_target_pairs={{0,1},{1,0},{2,3},{3,2},{4,5},{5,4},{6,7},{7,6},{8,9},{9,8},{10,11... | collective-permute-start | bytes 2752520 | tf_op jit(solution)/shard_map/ppermute | solution.py:48
  42.5 4.6 %collective-permute-start.13 = (f32[3,8,64]{2,1,0:T(8,128)S(1)}, f32[3,8,64]{2,1,0:T(8,128)S(1)}, u32[]{:S(2)}, u32[]{:S(2)}) collective-permute-start(f32[3,8,64]{2,1,0:T(8,128)S(1)} %add_select_fusion.2), channel_id=1, source_target_pairs={{0,6},{1,7},{2,4},{3,5},{4,2},{5,3},{6,0},{7,1},{8,14},{9,15},{10,... | collective-permute-start | bytes 18440 | tf_op jit(solution)/shard_map/ppermute | solution.py:183
  45.0 3.7 %collective-permute-start.12 = (f32[3,8,64]{2,1,0:T(8,128)S(1)}, f32[3,8,64]{2,1,0:T(8,128)S(1)}, u32[]{:S(2)}, u32[]{:S(2)}) collective-permute-start(f32[3,8,64]{2,1,0:T(8,128)S(1)} %add_select_fusion.2), channel_id=1, source_target_pairs={{0,4},{1,5},{2,6},{3,7},{4,0},{5,1},{6,2},{7,3},{8,12},{9,13},{10,... | collective-permute-start | bytes 18440 | tf_op jit(solution)/shard_map/ppermute | solution.py:183
  49.3 5.7 %collective-permute-start.16 = (f32[3,8,64]{2,1,0:T(8,128)S(1)}, f32[3,8,64]{2,1,0:T(8,128)S(1)}, u32[]{:S(2)}, u32[]{:S(2)}) collective-permute-start(f32[3,8,64]{2,1,0:T(8,128)S(1)} %add_select_fusion.1), channel_id=1, source_target_pairs={{0,24},{1,25},{2,26},{3,27},{4,28},{5,29},{6,30},{7,31},{8,16},{9,... | collective-permute-start | bytes 18440 | tf_op jit(solution)/shard_map/ppermute | solution.py:183
  52.8 4.6 %collective-permute-start.15 = (f32[3,8,64]{2,1,0:T(8,128)S(1)}, f32[3,8,64]{2,1,0:T(8,128)S(1)}, u32[]{:S(2)}, u32[]{:S(2)}) collective-permute-start(f32[3,8,64]{2,1,0:T(8,128)S(1)} %add_select_fusion.1), channel_id=1, source_target_pairs={{0,16},{1,17},{2,18},{3,19},{4,20},{5,21},{6,22},{7,23},{8,24},{9,... | collective-permute-start | bytes 18440 | tf_op jit(solution)/shard_map/ppermute | solution.py:183
  52.8 4.6 %collective-permute-start.14 = (f32[3,8,64]{2,1,0:T(8,128)S(1)}, f32[3,8,64]{2,1,0:T(8,128)S(1)}, u32[]{:S(2)}, u32[]{:S(2)}) collective-permute-start(f32[3,8,64]{2,1,0:T(8,128)S(1)} %add_select_fusion.1), channel_id=1, source_target_pairs={{0,8},{1,9},{2,10},{3,11},{4,12},{5,13},{6,14},{7,15},{8,0},{9,1},... | collective-permute-start | bytes 18440 | tf_op jit(solution)/shard_map/ppermute | solution.py:183
  62.0 5.7 %collective-permute-start.22 = (bf16[128,3584]{1,0:T(8,128)(2,1)S(1)}, bf16[128,3584]{1,0:T(8,128)(2,1)S(1)}, u32[]{:S(2)}, u32[]{:S(2)}) collective-permute-start(bf16[128,3584]{1,0:T(8,128)(2,1)S(1)} %get-tuple-element.20), channel_id=1, source_target_pairs={{0,1},{1,0},{2,3},{3,2},{4,5},{5,4},{6,7},{7,6},{8,9},{9,8},{10,11... | collective-permute-start | bytes 2752520 | tf_op jit(solution)/shard_map/ppermute | solution.py:48
  62.3 7.2 %collective-permute-start.17 = (bf16[128,3584]{1,0:T(8,128)(2,1)S(1)}, bf16[128,3584]{1,0:T(8,128)(2,1)S(1)}, u32[]{:S(2)}, u32[]{:S(2)}) collective-permute-start(bf16[128,3584]{1,0:T(8,128)(2,1)S(1)} %get-tuple-element.19), channel_id=1, source_target_pairs={{0,1},{1,0},{2,3},{3,2},{4,5},{5,4},{6,7},{7,6},{8,9},{9,8},{10,11... | collective-permute-start | bytes 2752520 | tf_op jit(solution)/shard_map/ppermute | solution.py:48
  67.9 8.5 %collective-permute-start.23 = (bf16[64,3584]{1,0:T(8,128)(2,1)S(1)}, bf16[64,3584]{1,0:T(8,128)(2,1)S(1)}, u32[]{:S(2)}, u32[]{:S(2)}) collective-permute-start(bf16[64,3584]{1,0:T(8,128)(2,1)S(1)} %slice.99), channel_id=1, source_target_pairs={{0,4},{1,3},{2,6},{3,1},{4,0},{5,7},{6,2},{7,5},{8,12},{9,11},{10,... | collective-permute-start | bytes 1376264 | tf_op jit(solution)/shard_map/ppermute | solution.py:44
  69.7 14.1 %collective-permute-start.18 = (bf16[64,3584]{1,0:T(8,128)(2,1)S(1)}, bf16[64,3584]{1,0:T(8,128)(2,1)S(1)}, u32[]{:S(2)}, u32[]{:S(2)}) collective-permute-start(bf16[64,3584]{1,0:T(8,128)(2,1)S(1)} %slice.91), channel_id=1, source_target_pairs={{0,4},{1,3},{2,6},{3,1},{4,0},{5,7},{6,2},{7,5},{8,12},{9,11},{10,... | collective-permute-start | bytes 1376264 | tf_op jit(solution)/shard_map/ppermute | solution.py:44
  76.6 8.0 %collective-permute-start.24 = (bf16[32,3584]{1,0:T(8,128)(2,1)S(1)}, bf16[32,3584]{1,0:T(8,128)(2,1)S(1)}, u32[]{:S(2)}, u32[]{:S(2)}) collective-permute-start(bf16[32,3584]{1,0:T(8,128)(2,1)S(1)} %slice.101), channel_id=1, source_target_pairs={{0,2},{1,5},{2,0},{3,7},{4,6},{5,1},{6,4},{7,3},{8,10},{9,13},{10,... | collective-permute-start | bytes 688136 | tf_op jit(solution)/shard_map/ppermute | solution.py:44
  84.0 6.1 %collective-permute-start.19 = (bf16[32,3584]{1,0:T(8,128)(2,1)S(1)}, bf16[32,3584]{1,0:T(8,128)(2,1)S(1)}, u32[]{:S(2)}, u32[]{:S(2)}) collective-permute-start(bf16[32,3584]{1,0:T(8,128)(2,1)S(1)} %slice.93), channel_id=1, source_target_pairs={{0,2},{1,5},{2,0},{3,7},{4,6},{5,1},{6,4},{7,3},{8,10},{9,13},{10,... | collective-permute-start | bytes 688136 | tf_op jit(solution)/shard_map/ppermute | solution.py:44
  84.6 6.8 %collective-permute-start.25 = (bf16[16,3584]{1,0:T(8,128)(2,1)S(1)}, bf16[16,3584]{1,0:T(8,128)(2,1)S(1)}, u32[]{:S(2)}, u32[]{:S(2)}) collective-permute-start(bf16[16,3584]{1,0:T(8,128)(2,1)S(1)} %slice.103), channel_id=1, source_target_pairs={{0,8},{1,17},{2,10},{3,19},{4,12},{5,21},{6,14},{7,23},{8,0},{9,25... | collective-permute-start | bytes 344072 | tf_op jit(solution)/shard_map/ppermute | solution.py:44
  90.1 5.3 %collective-permute-start.20 = (bf16[16,3584]{1,0:T(8,128)(2,1)S(1)}, bf16[16,3584]{1,0:T(8,128)(2,1)S(1)}, u32[]{:S(2)}, u32[]{:S(2)}) collective-permute-start(bf16[16,3584]{1,0:T(8,128)(2,1)S(1)} %slice.95), channel_id=1, source_target_pairs={{0,8},{1,17},{2,10},{3,19},{4,12},{5,21},{6,14},{7,23},{8,0},{9,25... | collective-permute-start | bytes 344072 | tf_op jit(solution)/shard_map/ppermute | solution.py:44
  91.5 6.2 %collective-permute-start.26 = (bf16[8,3584]{1,0:T(8,128)(2,1)S(1)}, bf16[8,3584]{1,0:T(8,128)(2,1)S(1)}, u32[]{:S(2)}, u32[]{:S(2)}) collective-permute-start(bf16[8,3584]{1,0:T(8,128)(2,1)S(1)} %slice.105), channel_id=1, source_target_pairs={{0,16},{1,9},{2,18},{3,11},{4,20},{5,13},{6,22},{7,15},{8,24},{9,1... | collective-permute-start | bytes 172040 | tf_op jit(solution)/shard_map/ppermute | solution.py:44
  95.5 5.4 %collective-permute-start.21 = (bf16[8,3584]{1,0:T(8,128)(2,1)S(1)}, bf16[8,3584]{1,0:T(8,128)(2,1)S(1)}, u32[]{:S(2)}, u32[]{:S(2)}) collective-permute-start(bf16[8,3584]{1,0:T(8,128)(2,1)S(1)} %slice.97), channel_id=1, source_target_pairs={{0,16},{1,9},{2,18},{3,11},{4,20},{5,13},{6,22},{7,15},{8,24},{9,1... | collective-permute-start | bytes 172040 | tf_op jit(solution)/shard_map/ppermute | solution.py:44
  (5 other events, 39.8 us)
where the time goes:
time: 102 us
  waiting for transfers between devices  54.2 us (53%)
  starting transfers between devices  29.6 us (29%)
  matrix products  11.6 us (11%)
  other arithmetic  1.9 us (2%)
  Pallas kernels  1.68 us (2%)
  local copies, waits for them, and re-layouts  1.58 us (2%)
    ppermute x16, waiting for transfers between devices, swap(): return lax.ppermute(value, AXIS, pairs)  46.5 us
    ppermute x16, starting transfers between devices, swap(): return lax.ppermute(value, AXIS, pairs)  20.2 us
    dot_general x7, matrix products, matmul(): lax.dot_general(left, right, (contract, ((), ())), preferred_element_type...  11.6 us
    ppermute x6, starting transfers between devices, exchange_stats(): lax.ppermute(stats, AXIS, [(i, i ^ mask) for i in range(size)])  7.96 us
    ppermute x6, waiting for transfers between devices, exchange_stats(): lax.ppermute(stats, AXIS, [(i, i ^ mask) for i in range(size)])  6.86 us
  transfers between devices with their start and end apart: 27, of which 17 were waited for; matrix products, arithmetic and copies ran while one was open for 9% of the time, Pallas kernels for 0%

commit v1 on v0

--- a/solution.py
+++ b/solution.py
@@ -20,7 +20,9 @@
         pair = bits[start : start + 2]
         low += pair if start == 0 else pair[::-1]
         high += pair[::-1] if start == 0 else pair
-    return [[low, high] for _ in range(groups)]
+    half = len(bits) // 2
+    other = [[*order[: half - 1], order[half], order[half - 1], *order[half + 1 :]] for order in (low, high)]
+    return [other if group % 2 == 1 else [low, high] for group in range(groups)]
 
 
 def masks_of(order):
@@ -86,13 +88,8 @@
     half = len(masks[0][0])
     size = 2 * half
     log_norm, mass, cross = stats_ref[0], stats_ref[1], stats_ref[2]
-    loss = mass * log_norm - cross
+    loss_ref[...] = mass * log_norm - cross
     lane = lax.broadcasted_iota(jnp.int32, mass.shape, 1)
-    square = (ROW_TILE, ROW_TILE)
-    diagonal = lax.broadcasted_iota(jnp.int32, square, 0) == lax.broadcasted_iota(jnp.int32, square, 1)
-    for group in range(groups):
-        column = jnp.sum(jnp.where(lane == group * size + me, loss, 0.0), axis=1, keepdims=True)
-        loss_ref[pl.ds(group, 1), :] = jnp.sum(jnp.where(diagonal, column, 0.0), axis=0, keepdims=True)
     for block in range(size):
         source = own_refs if block < half else pair_refs
         result = own_grad_ref if block < half else pair_grad_ref
@@ -106,6 +103,19 @@
             target = teacher_ref[group, pl.ds(start, ROW_TILE), :].astype(jnp.float32)
             grad = mass_rows * jnp.exp(logits - norm_rows) - target
             result[pl.ds((group * half + block % half) * ROW_TILE, ROW_TILE), :] = grad.astype(jnp.bfloat16)
+
+
+def own_loss_kernel(me_ref, all_ref, out_ref):
+    me = me_ref[0]
+    groups = out_ref.shape[0]
+    every = all_ref[...]
+    size = every.shape[1] // groups
+    lane = lax.broadcasted_iota(jnp.int32, every.shape, 1)
+    square = (ROW_TILE, ROW_TILE)
+    diagonal = lax.broadcasted_iota(jnp.int32, square, 0) == lax.broadcasted_iota(jnp.int32, square, 1)
+    for group in range(groups):
+        column = jnp.sum(jnp.where(lane == group * size + me, every, 0.0), axis=1, keepdims=True)
+        out_ref[pl.ds(group, 1), :] = jnp.sum(jnp.where(diagonal, column, 0.0), axis=0, keepdims=True)
 
 
 def vmem(count):
@@ -125,12 +135,24 @@
     )(me, teacher, *own, *pair)
 
 
+def call_own_loss(me, every, groups):
+    return pl.pallas_call(
+        own_loss_kernel,
+        out_shape=jax.ShapeDtypeStruct((groups, ROW_TILE), jnp.float32),
+        in_specs=[pl.BlockSpec(memory_space=pltpu.SMEM)] + vmem(1),
+        out_specs=vmem(1)[0],
+        cost_estimate=pl.CostEstimate(flops=1000, bytes_accessed=2000, transcendentals=0),
+        compiler_params=pltpu.CompilerParams(vmem_limit_bytes=VMEM_BYTES),
+        name="own_loss",
+    )(me, every)
+
+
 def call_grad(me, stats, own, pair, teacher, masks):
     groups = len(own)
     grad = jax.ShapeDtypeStruct((groups * own[0].shape[0], own[0].shape[1]), jnp.bfloat16)
     return pl.pallas_call(
         functools.partial(grad_kernel, masks),
-        out_shape=[jax.ShapeDtypeStruct((groups, ROW_TILE), jnp.float32), grad, grad],
+        out_shape=[jax.ShapeDtypeStruct(stats.shape[1:], jnp.float32), grad, grad],
         in_specs=[pl.BlockSpec(memory_space=pltpu.SMEM)] + vmem(2 * groups + 2),
         out_specs=vmem(3),
         cost_estimate=pl.CostEstimate(flops=2_000_000, bytes_accessed=3_200_000, transcendentals=400_000),
@@ -219,6 +241,7 @@
     if row_count == ROW_TILE:
         stats = exchange_stats(call_stats(me.reshape(1), own, pair, teacher, masks), size)
         loss, own_grad, pair_grad = call_grad(me.reshape(1), stats, own, pair, teacher, masks)
+        loss = call_own_loss(me.reshape(1), loss, groups)
     else:
         owners = [jnp.stack([owner_of(me, masks[group], block) for block in range(size)]) for group in range(groups)]
         blocks = teacher.reshape(groups, size, row_count, width)

time: 102 us -> 97.7 us (0.958)
  starting transfers between devices: 29.6 us -> 25.9 us
    ppermute x16, starting transfers between devices: 20.2 us -> 16.7 us  [swap(): return lax.ppermute(value, AXIS, pairs)]
  transfers between devices with their start and end apart: 27 -> 27, of which waited for: 17 -> 21; matrix products, arithmetic and copies ran while one was open for 9% -> 9% of each run, Pallas kernels for 0% -> 1%
where the time goes in v1:
time: 97.7 us; the launch traced here: 97.5 us
  waiting for transfers between devices  53.7 us (55%)
  starting transfers between devices  25.9 us (27%)
  matrix products  11.6 us (12%)
  other arithmetic  1.9 us (2%)
  Pallas kernels  1.76 us (2%)
  local copies, waits for them, and re-layouts  1.58 us (2%)
    ppermute x16, waiting for transfers between devices, swap(): return lax.ppermute(value, AXIS, pairs)  46.2 us
    ppermute x16, starting transfers between devices, swap(): return lax.ppermute(value, AXIS, pairs)  16.7 us
    dot_general x7, matrix products, matmul(): lax.dot_general(left, right, (contract, ((), ())), preferred_element_type...  11.6 us
    ppermute x6, starting transfers between devices, exchange_stats(): lax.ppermute(stats, AXIS, [(i, i ^ mask) for i in range(size)])  7.96 us
    ppermute x6, waiting for transfers between devices, exchange_stats(): lax.ppermute(stats, AXIS, [(i, i ^ mask) for i in range(size)])  6.67 us
  transfers between devices with their start and end apart: 27, of which 21 were waited for; matrix products, arithmetic and copies ran while one was open for 9% of the time, Pallas kernels for 1%

profile of v1, /device:TPU:0, one launch (start us, length us, event | category | flops | bytes accessed | tf_op | source)
XLA Modules:
  0.0 97.5 jit_solution(17787808468697217224)
XLA Ops:
  1.5 4.1 %collective-permute-start = (bf16[8,3584]{1,0:T(8,128)(2,1)S(1)}, bf16[8,3584]{1,0:T(8,128)(2,1)S(1)}, u32[]{:S(2)}, u32[]{:S(2)}) collective-permute-start(bf16[8,3584]{1,0:T(8,128)(2,1)S(1)} %get-tuple-element.22), channel_id=1, source_target_pairs={{0,16},{1,9},{2,18},{3,11},{4,20},{5,13},{6,22},{7,15},{8,24},{9,1... | collective-permute-start | bytes 172040 | tf_op jit(solution)/shard_map/ppermute | solution.py:46
  5.7 2.2 %collective-permute-done = bf16[8,3584]{1,0:T(8,128)(2,1)S(1)} collective-permute-done((bf16[8,3584]{1,0:T(8,128)(2,1)S(1)}, bf16[8,3584]{1,0:T(8,128)(2,1)S(1)}, u32[]{:S(2)}, u32[]{:S(2)}) %collective-permute-start) | collective-permute-done | bytes 57376 | tf_op jit(solution)/shard_map/ppermute | solution.py:46
  7.9 2.2 %collective-permute-start.1 = (bf16[16,3584]{1,0:T(8,128)(2,1)S(1)}, bf16[16,3584]{1,0:T(8,128)(2,1)S(1)}, u32[]{:S(2)}, u32[]{:S(2)}) collective-permute-start(bf16[16,3584]{1,0:T(8,128)(2,1)S(1)} %pad_maximum_fusion.6), channel_id=1, source_target_pairs={{0,8},{1,17},{2,10},{3,19},{4,12},{5,21},{6,14},{7,23},{8,0},{9,25... | collective-permute-start | bytes 344072 | tf_op jit(solution)/shard_map/ppermute | solution.py:46
  10.1 3.1 %collective-permute-done.4 = bf16[8,3584]{1,0:T(8,128)(2,1)S(1)} collective-permute-done((bf16[8,3584]{1,0:T(8,128)(2,1)S(1)}, bf16[8,3584]{1,0:T(8,128)(2,1)S(1)}, u32[]{:S(2)}, u32[]{:S(2)}) %collective-permute-start.4) | collective-permute-done | bytes 57376 | tf_op jit(solution)/shard_map/ppermute | solution.py:46
  15.4 2.7 %collective-permute-done.5 = bf16[16,3584]{1,0:T(8,128)(2,1)S(1)} collective-permute-done((bf16[16,3584]{1,0:T(8,128)(2,1)S(1)}, bf16[16,3584]{1,0:T(8,128)(2,1)S(1)}, u32[]{:S(2)}, u32[]{:S(2)}) %collective-permute-start.5) | collective-permute-done | bytes 114720 | tf_op jit(solution)/shard_map/ppermute | solution.py:46
  18.2 2.7 %collective-permute-done.2 = bf16[32,3584]{1,0:T(8,128)(2,1)S(1)} collective-permute-done((bf16[32,3584]{1,0:T(8,128)(2,1)S(1)}, bf16[32,3584]{1,0:T(8,128)(2,1)S(1)}, u32[]{:S(2)}, u32[]{:S(2)}) %collective-permute-start.2) | collective-permute-done | bytes 229408 | tf_op jit(solution)/shard_map/ppermute | solution.py:46
  21.0 1.6 %collective-permute-start.3 = (bf16[64,3584]{1,0:T(8,128)(2,1)S(1)}, bf16[64,3584]{1,0:T(8,128)(2,1)S(1)}, u32[]{:S(2)}, u32[]{:S(2)}) collective-permute-start(bf16[64,3584]{1,0:T(8,128)(2,1)S(1)} %pad_maximum_fusion.2), channel_id=1, source_target_pairs={{0,4},{1,3},{2,6},{3,1},{4,0},{5,7},{6,2},{7,5},{8,12},{9,11},{10,... | collective-permute-start | bytes 1376264 | tf_op jit(solution)/shard_map/ppermute | solution.py:46
  22.5 2.8 %collective-permute-done.6 = bf16[32,3584]{1,0:T(8,128)(2,1)S(1)} collective-permute-done((bf16[32,3584]{1,0:T(8,128)(2,1)S(1)}, bf16[32,3584]{1,0:T(8,128)(2,1)S(1)}, u32[]{:S(2)}, u32[]{:S(2)}) %collective-permute-start.6) | collective-permute-done | bytes 229408 | tf_op jit(solution)/shard_map/ppermute | solution.py:46
  26.0 3.5 %collective-permute-done.3 = bf16[64,3584]{1,0:T(8,128)(2,1)S(1)} collective-permute-done((bf16[64,3584]{1,0:T(8,128)(2,1)S(1)}, bf16[64,3584]{1,0:T(8,128)(2,1)S(1)}, u32[]{:S(2)}, u32[]{:S(2)}) %collective-permute-start.3) | collective-permute-done | bytes 458784 | tf_op jit(solution)/shard_map/ppermute | solution.py:46
  29.6 4.8 %collective-permute-done.7 = bf16[64,3584]{1,0:T(8,128)(2,1)S(1)} collective-permute-done((bf16[64,3584]{1,0:T(8,128)(2,1)S(1)}, bf16[64,3584]{1,0:T(8,128)(2,1)S(1)}, u32[]{:S(2)}, u32[]{:S(2)}) %collective-permute-start.7) | collective-permute-done | bytes 458784 | tf_op jit(solution)/shard_map/ppermute | solution.py:46
  40.5 2.1 %collective-permute-start.13 = (f32[3,8,64]{2,1,0:T(8,128)S(1)}, f32[3,8,64]{2,1,0:T(8,128)S(1)}, u32[]{:S(2)}, u32[]{:S(2)}) collective-permute-start(f32[3,8,64]{2,1,0:T(8,128)S(1)} %add_select_fusion.2), channel_id=1, source_target_pairs={{0,6},{1,7},{2,4},{3,5},{4,2},{5,3},{6,0},{7,1},{8,14},{9,15},{10,... | collective-permute-start | bytes 18440 | tf_op jit(solution)/shard_map/ppermute | solution.py:205
  47.0 3.7 %collective-permute-start.16 = (f32[3,8,64]{2,1,0:T(8,128)S(1)}, f32[3,8,64]{2,1,0:T(8,128)S(1)}, u32[]{:S(2)}, u32[]{:S(2)}) collective-permute-start(f32[3,8,64]{2,1,0:T(8,128)S(1)} %add_select_fusion.1), channel_id=1, source_target_pairs={{0,24},{1,25},{2,26},{3,27},{4,28},{5,29},{6,30},{7,31},{8,16},{9,... | collective-permute-start | bytes 18440 | tf_op jit(solution)/shard_map/ppermute | solution.py:205
  52.5 2.8 %collective-permute-done.15 = f32[3,8,64]{2,1,0:T(8,128)S(1)} collective-permute-done((f32[3,8,64]{2,1,0:T(8,128)S(1)}, f32[3,8,64]{2,1,0:T(8,128)S(1)}, u32[]{:S(2)}, u32[]{:S(2)}) %collective-permute-start.15) | collective-permute-done | bytes 6176 | tf_op jit(solution)/shard_map/ppermute | solution.py:205
  55.8 1.6 %convolution_convert_fusion.1 = bf16[256,3584]{1,0:T(8,128)(2,1)S(1)} fusion(bf16[256,768]{1,0:T(8,128)(2,1)S(1)} %get-tuple-element.11, bf16[3584,768]{1,0:T(8,128)(2,1)S(1)} %copy-done.1), kind=kOutput, calls=%fused_computation.1 | convolution fusion | flops 1410203648 | bytes 7733248 | tf_op jit(solution)/shard_map/dot_general | solution.py:212
  57.5 1.6 %fusion.19 = f32[256,3584]{1,0:T(8,128)S(1)} fusion(bf16[256,768]{1,0:T(8,128)(2,1)S(1)} %get-tuple-element.13, bf16[3584,768]{1,0:T(8,128)(2,1)S(1)} %copy-done.1), kind=kOutput, calls=%fused_computation.46 | convolution fusion | flops 1409286144 | bytes 9568256 | tf_op jit(solution)/shard_map/dot_general | solution.py:212
  60.7 4.8 %convolution_convert_fusion = bf16[3584,768]{1,0:T(8,128)(2,1)} fusion(bf16[128,3584]{1,0:T(8,128)(2,1)S(1)} %collective-permute-done.9, bf16[128,3584]{1,0:T(8,128)(2,1)S(1)} %collective-permute-done.8, bf16[128,3584]{1,0:T(8,128)(2,1)S(1)} %pad_maximum_fusion.1, bf16[128,3584]{1,0:T(8,128)(2,1)S(1)} %pad_maximum_fusion, ...), kind=kOutput, calls=%fused_computation | convolution fusion | flops 2837577728 | bytes 9961472 | tf_op jit(solution)/shard_map/dot_general | solution.py:212
  65.8 1.6 %collective-permute-start.23 = (bf16[64,3584]{1,0:T(8,128)(2,1)S(1)}, bf16[64,3584]{1,0:T(8,128)(2,1)S(1)}, u32[]{:S(2)}, u32[]{:S(2)}) collective-permute-start(bf16[64,3584]{1,0:T(8,128)(2,1)S(1)} %slice.99), channel_id=1, source_target_pairs={{0,4},{1,3},{2,6},{3,1},{4,0},{5,7},{6,2},{7,5},{8,12},{9,11},{10,... | collective-permute-start | bytes 1376264 | tf_op jit(solution)/shard_map/ppermute | solution.py:46
  68.1 6.2 %collective-permute-done.23 = bf16[64,3584]{1,0:T(8,128)(2,1)S(1)} collective-permute-done((bf16[64,3584]{1,0:T(8,128)(2,1)S(1)}, bf16[64,3584]{1,0:T(8,128)(2,1)S(1)}, u32[]{:S(2)}, u32[]{:S(2)}) %collective-permute-start.23) | collective-permute-done | bytes 458784 | tf_op jit(solution)/shard_map/ppermute | solution.py:46
  74.5 4.7 %collective-permute-done.18 = bf16[64,3584]{1,0:T(8,128)(2,1)S(1)} collective-permute-done((bf16[64,3584]{1,0:T(8,128)(2,1)S(1)}, bf16[64,3584]{1,0:T(8,128)(2,1)S(1)}, u32[]{:S(2)}, u32[]{:S(2)}) %collective-permute-start.18) | collective-permute-done | bytes 458784 | tf_op jit(solution)/shard_map/ppermute | solution.py:46
  80.0 2.9 %collective-permute-done.24 = bf16[32,3584]{1,0:T(8,128)(2,1)S(1)} collective-permute-done((bf16[32,3584]{1,0:T(8,128)(2,1)S(1)}, bf16[32,3584]{1,0:T(8,128)(2,1)S(1)}, u32[]{:S(2)}, u32[]{:S(2)}) %collective-permute-start.24) | collective-permute-done | bytes 229408 | tf_op jit(solution)/shard_map/ppermute | solution.py:46
  83.6 1.9 %collective-permute-done.19 = bf16[32,3584]{1,0:T(8,128)(2,1)S(1)} collective-permute-done((bf16[32,3584]{1,0:T(8,128)(2,1)S(1)}, bf16[32,3584]{1,0:T(8,128)(2,1)S(1)}, u32[]{:S(2)}, u32[]{:S(2)}) %collective-permute-start.19) | collective-permute-done | bytes 229408 | tf_op jit(solution)/shard_map/ppermute | solution.py:46
  85.6 2.2 %collective-permute-done.25 = bf16[16,3584]{1,0:T(8,128)(2,1)S(1)} collective-permute-done((bf16[16,3584]{1,0:T(8,128)(2,1)S(1)}, bf16[16,3584]{1,0:T(8,128)(2,1)S(1)}, u32[]{:S(2)}, u32[]{:S(2)}) %collective-permute-start.25) | collective-permute-done | bytes 114720 | tf_op jit(solution)/shard_map/ppermute | solution.py:46
  88.8 2.2 %collective-permute-done.20 = bf16[16,3584]{1,0:T(8,128)(2,1)S(1)} collective-permute-done((bf16[16,3584]{1,0:T(8,128)(2,1)S(1)}, bf16[16,3584]{1,0:T(8,128)(2,1)S(1)}, u32[]{:S(2)}, u32[]{:S(2)}) %collective-permute-start.20) | collective-permute-done | bytes 114720 | tf_op jit(solution)/shard_map/ppermute | solution.py:46
  93.1 3.7 %collective-permute-done.21 = bf16[8,3584]{1,0:T(8,128)(2,1)S(1)} collective-permute-done((bf16[8,3584]{1,0:T(8,128)(2,1)S(1)}, bf16[8,3584]{1,0:T(8,128)(2,1)S(1)}, u32[]{:S(2)}, u32[]{:S(2)}) %collective-permute-start.21) | collective-permute-done | bytes 57376 | tf_op jit(solution)/shard_map/ppermute | solution.py:46
  (78 shorter events, 24.7 us)
Async XLA Ops:
  1.5 6.4 %collective-permute-start = (bf16[8,3584]{1,0:T(8,128)(2,1)S(1)}, bf16[8,3584]{1,0:T(8,128)(2,1)S(1)}, u32[]{:S(2)}, u32[]{:S(2)}) collective-permute-start(bf16[8,3584]{1,0:T(8,128)(2,1)S(1)} %get-tuple-element.22), channel_id=1, source_target_pairs={{0,16},{1,9},{2,18},{3,11},{4,20},{5,13},{6,22},{7,15},{8,24},{9,1... | collective-permute-start | bytes 172040 | tf_op jit(solution)/shard_map/ppermute | solution.py:46
  5.6 7.6 %collective-permute-start.4 = (bf16[8,3584]{1,0:T(8,128)(2,1)S(1)}, bf16[8,3584]{1,0:T(8,128)(2,1)S(1)}, u32[]{:S(2)}, u32[]{:S(2)}) collective-permute-start(bf16[8,3584]{1,0:T(8,128)(2,1)S(1)} %get-tuple-element.21), channel_id=1, source_target_pairs={{0,16},{1,9},{2,18},{3,11},{4,20},{5,13},{6,22},{7,15},{8,24},{9,1... | collective-permute-start | bytes 172040 | tf_op jit(solution)/shard_map/ppermute | solution.py:46
  7.9 6.9 %collective-permute-start.1 = (bf16[16,3584]{1,0:T(8,128)(2,1)S(1)}, bf16[16,3584]{1,0:T(8,128)(2,1)S(1)}, u32[]{:S(2)}, u32[]{:S(2)}) collective-permute-start(bf16[16,3584]{1,0:T(8,128)(2,1)S(1)} %pad_maximum_fusion.6), channel_id=1, source_target_pairs={{0,8},{1,17},{2,10},{3,19},{4,12},{5,21},{6,14},{7,23},{8,0},{9,25... | collective-permute-start | bytes 344072 | tf_op jit(solution)/shard_map/ppermute | solution.py:46
  13.2 4.9 %collective-permute-start.5 = (bf16[16,3584]{1,0:T(8,128)(2,1)S(1)}, bf16[16,3584]{1,0:T(8,128)(2,1)S(1)}, u32[]{:S(2)}, u32[]{:S(2)}) collective-permute-start(bf16[16,3584]{1,0:T(8,128)(2,1)S(1)} %pad_maximum_fusion.7), channel_id=1, source_target_pairs={{0,2},{1,5},{2,0},{3,7},{4,6},{5,1},{6,4},{7,3},{8,10},{9,13},{10,... | collective-permute-start | bytes 344072 | tf_op jit(solution)/shard_map/ppermute | solution.py:46
  14.8 6.1 %collective-permute-start.2 = (bf16[32,3584]{1,0:T(8,128)(2,1)S(1)}, bf16[32,3584]{1,0:T(8,128)(2,1)S(1)}, u32[]{:S(2)}, u32[]{:S(2)}) collective-permute-start(bf16[32,3584]{1,0:T(8,128)(2,1)S(1)} %pad_maximum_fusion.4), channel_id=1, source_target_pairs={{0,2},{1,5},{2,0},{3,7},{4,6},{5,1},{6,4},{7,3},{8,10},{9,13},{10,... | collective-permute-start | bytes 688136 | tf_op jit(solution)/shard_map/ppermute | solution.py:46
  18.1 7.2 %collective-permute-start.6 = (bf16[32,3584]{1,0:T(8,128)(2,1)S(1)}, bf16[32,3584]{1,0:T(8,128)(2,1)S(1)}, u32[]{:S(2)}, u32[]{:S(2)}) collective-permute-start(bf16[32,3584]{1,0:T(8,128)(2,1)S(1)} %pad_maximum_fusion.5), channel_id=1, source_target_pairs={{0,8},{1,17},{2,10},{3,19},{4,12},{5,21},{6,14},{7,23},{8,0},{9,25... | collective-permute-start | bytes 688136 | tf_op jit(solution)/shard_map/ppermute | solution.py:46
  21.0 8.5 %collective-permute-start.3 = (bf16[64,3584]{1,0:T(8,128)(2,1)S(1)}, bf16[64,3584]{1,0:T(8,128)(2,1)S(1)}, u32[]{:S(2)}, u32[]{:S(2)}) collective-permute-start(bf16[64,3584]{1,0:T(8,128)(2,1)S(1)} %pad_maximum_fusion.2), channel_id=1, source_target_pairs={{0,4},{1,3},{2,6},{3,1},{4,0},{5,7},{6,2},{7,5},{8,12},{9,11},{10,... | collective-permute-start | bytes 1376264 | tf_op jit(solution)/shard_map/ppermute | solution.py:46
  25.4 9.0 %collective-permute-start.7 = (bf16[64,3584]{1,0:T(8,128)(2,1)S(1)}, bf16[64,3584]{1,0:T(8,128)(2,1)S(1)}, u32[]{:S(2)}, u32[]{:S(2)}) collective-permute-start(bf16[64,3584]{1,0:T(8,128)(2,1)S(1)} %pad_maximum_fusion.3), channel_id=1, source_target_pairs={{0,4},{1,3},{2,6},{3,1},{4,0},{5,7},{6,2},{7,5},{8,12},{9,11},{10,... | collective-permute-start | bytes 1376264 | tf_op jit(solution)/shard_map/ppermute | solution.py:46
  29.6 6.8 %collective-permute-start.8 = (bf16[128,3584]{1,0:T(8,128)(2,1)S(1)}, bf16[128,3584]{1,0:T(8,128)(2,1)S(1)}, u32[]{:S(2)}, u32[]{:S(2)}) collective-permute-start(bf16[128,3584]{1,0:T(8,128)(2,1)S(1)} %pad_maximum_fusion), channel_id=1, source_target_pairs={{0,1},{1,0},{2,3},{3,2},{4,5},{5,4},{6,7},{7,6},{8,9},{9,8},{10,11... | collective-permute-start | bytes 2752520 | tf_op jit(solution)/shard_map/ppermute | solution.py:50
  40.5 4.6 %collective-permute-start.13 = (f32[3,8,64]{2,1,0:T(8,128)S(1)}, f32[3,8,64]{2,1,0:T(8,128)S(1)}, u32[]{:S(2)}, u32[]{:S(2)}) collective-permute-start(f32[3,8,64]{2,1,0:T(8,128)S(1)} %add_select_fusion.2), channel_id=1, source_target_pairs={{0,6},{1,7},{2,4},{3,5},{4,2},{5,3},{6,0},{7,1},{8,14},{9,15},{10,... | collective-permute-start | bytes 18440 | tf_op jit(solution)/shard_map/ppermute | solution.py:205
  42.6 3.7 %collective-permute-start.12 = (f32[3,8,64]{2,1,0:T(8,128)S(1)}, f32[3,8,64]{2,1,0:T(8,128)S(1)}, u32[]{:S(2)}, u32[]{:S(2)}) collective-permute-start(f32[3,8,64]{2,1,0:T(8,128)S(1)} %add_select_fusion.2), channel_id=1, source_target_pairs={{0,4},{1,5},{2,6},{3,7},{4,0},{5,1},{6,2},{7,3},{8,12},{9,13},{10,... | collective-permute-start | bytes 18440 | tf_op jit(solution)/shard_map/ppermute | solution.py:205
  47.0 5.6 %collective-permute-start.16 = (f32[3,8,64]{2,1,0:T(8,128)S(1)}, f32[3,8,64]{2,1,0:T(8,128)S(1)}, u32[]{:S(2)}, u32[]{:S(2)}) collective-permute-start(f32[3,8,64]{2,1,0:T(8,128)S(1)} %add_select_fusion.1), channel_id=1, source_target_pairs={{0,24},{1,25},{2,26},{3,27},{4,28},{5,29},{6,30},{7,31},{8,16},{9,... | collective-permute-start | bytes 18440 | tf_op jit(solution)/shard_map/ppermute | solution.py:205
  50.7 4.6 %collective-permute-start.15 = (f32[3,8,64]{2,1,0:T(8,128)S(1)}, f32[3,8,64]{2,1,0:T(8,128)S(1)}, u32[]{:S(2)}, u32[]{:S(2)}) collective-permute-start(f32[3,8,64]{2,1,0:T(8,128)S(1)} %add_select_fusion.1), channel_id=1, source_target_pairs={{0,16},{1,17},{2,18},{3,19},{4,20},{5,21},{6,22},{7,23},{8,24},{9,... | collective-permute-start | bytes 18440 | tf_op jit(solution)/shard_map/ppermute | solution.py:205
  50.7 4.6 %collective-permute-start.14 = (f32[3,8,64]{2,1,0:T(8,128)S(1)}, f32[3,8,64]{2,1,0:T(8,128)S(1)}, u32[]{:S(2)}, u32[]{:S(2)}) collective-permute-start(f32[3,8,64]{2,1,0:T(8,128)S(1)} %add_select_fusion.1), channel_id=1, source_target_pairs={{0,8},{1,9},{2,10},{3,11},{4,12},{5,13},{6,14},{7,15},{8,0},{9,1},... | collective-permute-start | bytes 18440 | tf_op jit(solution)/shard_map/ppermute | solution.py:205
  59.3 6.3 %collective-permute-start.22 = (bf16[128,3584]{1,0:T(8,128)(2,1)S(1)}, bf16[128,3584]{1,0:T(8,128)(2,1)S(1)}, u32[]{:S(2)}, u32[]{:S(2)}) collective-permute-start(bf16[128,3584]{1,0:T(8,128)(2,1)S(1)} %get-tuple-element.20), channel_id=1, source_target_pairs={{0,1},{1,0},{2,3},{3,2},{4,5},{5,4},{6,7},{7,6},{8,9},{9,8},{10,11... | collective-permute-start | bytes 2752520 | tf_op jit(solution)/shard_map/ppermute | solution.py:50
  60.2 7.1 %collective-permute-start.17 = (bf16[128,3584]{1,0:T(8,128)(2,1)S(1)}, bf16[128,3584]{1,0:T(8,128)(2,1)S(1)}, u32[]{:S(2)}, u32[]{:S(2)}) collective-permute-start(bf16[128,3584]{1,0:T(8,128)(2,1)S(1)} %get-tuple-element.19), channel_id=1, source_target_pairs={{0,1},{1,0},{2,3},{3,2},{4,5},{5,4},{6,7},{7,6},{8,9},{9,8},{10,11... | collective-permute-start | bytes 2752520 | tf_op jit(solution)/shard_map/ppermute | solution.py:50
  65.8 8.5 %collective-permute-start.23 = (bf16[64,3584]{1,0:T(8,128)(2,1)S(1)}, bf16[64,3584]{1,0:T(8,128)(2,1)S(1)}, u32[]{:S(2)}, u32[]{:S(2)}) collective-permute-start(bf16[64,3584]{1,0:T(8,128)(2,1)S(1)} %slice.99), channel_id=1, source_target_pairs={{0,4},{1,3},{2,6},{3,1},{4,0},{5,7},{6,2},{7,5},{8,12},{9,11},{10,... | collective-permute-start | bytes 1376264 | tf_op jit(solution)/shard_map/ppermute | solution.py:46
  67.5 11.7 %collective-permute-start.18 = (bf16[64,3584]{1,0:T(8,128)(2,1)S(1)}, bf16[64,3584]{1,0:T(8,128)(2,1)S(1)}, u32[]{:S(2)}, u32[]{:S(2)}) collective-permute-start(bf16[64,3584]{1,0:T(8,128)(2,1)S(1)} %slice.91), channel_id=1, source_target_pairs={{0,4},{1,3},{2,6},{3,1},{4,0},{5,7},{6,2},{7,5},{8,12},{9,11},{10,... | collective-permute-start | bytes 1376264 | tf_op jit(solution)/shard_map/ppermute | solution.py:46
  74.4 8.5 %collective-permute-start.24 = (bf16[32,3584]{1,0:T(8,128)(2,1)S(1)}, bf16[32,3584]{1,0:T(8,128)(2,1)S(1)}, u32[]{:S(2)}, u32[]{:S(2)}) collective-permute-start(bf16[32,3584]{1,0:T(8,128)(2,1)S(1)} %slice.101), channel_id=1, source_target_pairs={{0,8},{1,17},{2,10},{3,19},{4,12},{5,21},{6,14},{7,23},{8,0},{9,25... | collective-permute-start | bytes 688136 | tf_op jit(solution)/shard_map/ppermute | solution.py:46
  79.4 6.1 %collective-permute-start.19 = (bf16[32,3584]{1,0:T(8,128)(2,1)S(1)}, bf16[32,3584]{1,0:T(8,128)(2,1)S(1)}, u32[]{:S(2)}, u32[]{:S(2)}) collective-permute-start(bf16[32,3584]{1,0:T(8,128)(2,1)S(1)} %slice.93), channel_id=1, source_target_pairs={{0,2},{1,5},{2,0},{3,7},{4,6},{5,1},{6,4},{7,3},{8,10},{9,13},{10,... | collective-permute-start | bytes 688136 | tf_op jit(solution)/shard_map/ppermute | solution.py:46
  83.0 4.9 %collective-permute-start.25 = (bf16[16,3584]{1,0:T(8,128)(2,1)S(1)}, bf16[16,3584]{1,0:T(8,128)(2,1)S(1)}, u32[]{:S(2)}, u32[]{:S(2)}) collective-permute-start(bf16[16,3584]{1,0:T(8,128)(2,1)S(1)} %slice.103), channel_id=1, source_target_pairs={{0,2},{1,5},{2,0},{3,7},{4,6},{5,1},{6,4},{7,3},{8,10},{9,13},{10,... | collective-permute-start | bytes 344072 | tf_op jit(solution)/shard_map/ppermute | solution.py:46
  85.5 5.5 %collective-permute-start.20 = (bf16[16,3584]{1,0:T(8,128)(2,1)S(1)}, bf16[16,3584]{1,0:T(8,128)(2,1)S(1)}, u32[]{:S(2)}, u32[]{:S(2)}) collective-permute-start(bf16[16,3584]{1,0:T(8,128)(2,1)S(1)} %slice.95), channel_id=1, source_target_pairs={{0,8},{1,17},{2,10},{3,19},{4,12},{5,21},{6,14},{7,23},{8,0},{9,25... | collective-permute-start | bytes 344072 | tf_op jit(solution)/shard_map/ppermute | solution.py:46
  87.9 5.2 %collective-permute-start.26 = (bf16[8,3584]{1,0:T(8,128)(2,1)S(1)}, bf16[8,3584]{1,0:T(8,128)(2,1)S(1)}, u32[]{:S(2)}, u32[]{:S(2)}) collective-permute-start(bf16[8,3584]{1,0:T(8,128)(2,1)S(1)} %slice.105), channel_id=1, source_target_pairs={{0,16},{1,9},{2,18},{3,11},{4,20},{5,13},{6,22},{7,15},{8,24},{9,1... | collective-permute-start | bytes 172040 | tf_op jit(solution)/shard_map/ppermute | solution.py:46
  91.0 5.8 %collective-permute-start.21 = (bf16[8,3584]{1,0:T(8,128)(2,1)S(1)}, bf16[8,3584]{1,0:T(8,128)(2,1)S(1)}, u32[]{:S(2)}, u32[]{:S(2)}) collective-permute-start(bf16[8,3584]{1,0:T(8,128)(2,1)S(1)} %slice.97), channel_id=1, source_target_pairs={{0,16},{1,9},{2,18},{3,11},{4,20},{5,13},{6,22},{7,15},{8,24},{9,1... | collective-permute-start | bytes 172040 | tf_op jit(solution)/shard_map/ppermute | solution.py:46
  (5 other events, 37.9 us)

commit v2 on v1

--- a/solution.py
+++ b/solution.py
@@ -15,14 +15,21 @@
 
 def stage_orders(size, groups):
     bits = list(range(size.bit_length() - 2, 0, -1))
-    low, high = [], []
-    for start in range(0, len(bits), 2):
-        pair = bits[start : start + 2]
-        low += pair if start == 0 else pair[::-1]
-        high += pair[::-1] if start == 0 else pair
     half = len(bits) // 2
-    other = [[*order[: half - 1], order[half], order[half - 1], *order[half + 1 :]] for order in (low, high)]
-    return [other if group % 2 == 1 else [low, high] for group in range(groups)]
+    walks = []
+    for group in range(groups):
+        odd = group % 2
+        low, high = [], []
+        for start in range(0, len(bits), 2):
+            pair = bits[start : start + 2]
+            turn = odd and start > 0
+            low += pair[::-1] if turn else pair
+            high += pair if turn else pair[::-1]
+        if odd and half:
+            for order in (low, high):
+                order[half - 1], order[half] = order[half], order[half - 1]
+        walks.append([low, high])
+    return walks
 
 
 def masks_of(order):

time: 97.7 us -> 98.6 us (level)
  starting transfers between devices: 25.9 us -> 30.5 us
  waiting for transfers between devices: 53.7 us -> 50.3 us
    ppermute x16, starting transfers between devices: 16.7 us -> 21.4 us  [swap(): return lax.ppermute(value, AXIS, pairs)]
    ppermute x16, waiting for transfers between devices: 46.2 us -> 43 us  [swap(): return lax.ppermute(value, AXIS, pairs)]
where the time goes in v2:
time: 98.6 us; the launch traced here: 98.5 us
  waiting for transfers between devices  50.3 us (51%)
  starting transfers between devices  30.5 us (31%)
  matrix products  11.6 us (12%)
  other arithmetic  1.9 us (2%)
  Pallas kernels  1.78 us (2%)
  local copies, waits for them, and re-layouts  1.36 us (1%)
    ppermute x16, waiting for transfers between devices, swap(): return lax.ppermute(value, AXIS, pairs)  43 us
    ppermute x16, starting transfers between devices, swap(): return lax.ppermute(value, AXIS, pairs)  21.4 us
    dot_general x7, matrix products, matmul(): lax.dot_general(left, right, (contract, ((), ())), preferred_element_type...  11.6 us
    ppermute x6, starting transfers between devices, exchange_stats(): lax.ppermute(stats, AXIS, [(i, i ^ mask) for i in range(size)])  7.97 us
    ppermute x6, waiting for transfers between devices, exchange_stats(): lax.ppermute(stats, AXIS, [(i, i ^ mask) for i in range(size)])  5.8 us
  transfers between devices with their start and end apart: 27, of which 21 were waited for; matrix products, arithmetic and copies ran while one was open for 9% of the time, Pallas kernels for 1%

profile of v2, /device:TPU:0, one launch (start us, length us, event | category | flops | bytes accessed | tf_op | source)
XLA Modules:
  0.0 98.5 jit_solution(2190876435609765143)
XLA Ops:
  1.5 4.1 %collective-permute-start = (bf16[8,3584]{1,0:T(8,128)(2,1)S(1)}, bf16[8,3584]{1,0:T(8,128)(2,1)S(1)}, u32[]{:S(2)}, u32[]{:S(2)}) collective-permute-start(bf16[8,3584]{1,0:T(8,128)(2,1)S(1)} %get-tuple-element.22), channel_id=1, source_target_pairs={{0,16},{1,9},{2,18},{3,11},{4,20},{5,13},{6,22},{7,15},{8,24},{9,1... | collective-permute-start | bytes 172040 | tf_op jit(solution)/shard_map/ppermute | solution.py:53
  5.7 2.2 %collective-permute-done = bf16[8,3584]{1,0:T(8,128)(2,1)S(1)} collective-permute-done((bf16[8,3584]{1,0:T(8,128)(2,1)S(1)}, bf16[8,3584]{1,0:T(8,128)(2,1)S(1)}, u32[]{:S(2)}, u32[]{:S(2)}) %collective-permute-start) | collective-permute-done | bytes 57376 | tf_op jit(solution)/shard_map/ppermute | solution.py:53
  7.9 2.2 %collective-permute-start.1 = (bf16[16,3584]{1,0:T(8,128)(2,1)S(1)}, bf16[16,3584]{1,0:T(8,128)(2,1)S(1)}, u32[]{:S(2)}, u32[]{:S(2)}) collective-permute-start(bf16[16,3584]{1,0:T(8,128)(2,1)S(1)} %pad_maximum_fusion.6), channel_id=1, source_target_pairs={{0,8},{1,17},{2,10},{3,19},{4,12},{5,21},{6,14},{7,23},{8,0},{9,25... | collective-permute-start | bytes 344072 | tf_op jit(solution)/shard_map/ppermute | solution.py:53
  10.1 3.1 %collective-permute-done.4 = bf16[8,3584]{1,0:T(8,128)(2,1)S(1)} collective-permute-done((bf16[8,3584]{1,0:T(8,128)(2,1)S(1)}, bf16[8,3584]{1,0:T(8,128)(2,1)S(1)}, u32[]{:S(2)}, u32[]{:S(2)}) %collective-permute-start.4) | collective-permute-done | bytes 57376 | tf_op jit(solution)/shard_map/ppermute | solution.py:53
  13.2 1.6 %collective-permute-start.5 = (bf16[16,3584]{1,0:T(8,128)(2,1)S(1)}, bf16[16,3584]{1,0:T(8,128)(2,1)S(1)}, u32[]{:S(2)}, u32[]{:S(2)}) collective-permute-start(bf16[16,3584]{1,0:T(8,128)(2,1)S(1)} %pad_maximum_fusion.7), channel_id=1, source_target_pairs={{0,2},{1,5},{2,0},{3,7},{4,6},{5,1},{6,4},{7,3},{8,10},{9,13},{10,... | collective-permute-start | bytes 344072 | tf_op jit(solution)/shard_map/ppermute | solution.py:53
  14.8 1.6 %collective-permute-start.2 = (bf16[32,3584]{1,0:T(8,128)(2,1)S(1)}, bf16[32,3584]{1,0:T(8,128)(2,1)S(1)}, u32[]{:S(2)}, u32[]{:S(2)}) collective-permute-start(bf16[32,3584]{1,0:T(8,128)(2,1)S(1)} %pad_maximum_fusion.4), channel_id=1, source_target_pairs={{0,4},{1,3},{2,6},{3,1},{4,0},{5,7},{6,2},{7,5},{8,12},{9,11},{10,... | collective-permute-start | bytes 688136 | tf_op jit(solution)/shard_map/ppermute | solution.py:53
  16.4 2.9 %collective-permute-done.5 = bf16[16,3584]{1,0:T(8,128)(2,1)S(1)} collective-permute-done((bf16[16,3584]{1,0:T(8,128)(2,1)S(1)}, bf16[16,3584]{1,0:T(8,128)(2,1)S(1)}, u32[]{:S(2)}, u32[]{:S(2)}) %collective-permute-start.5) | collective-permute-done | bytes 114720 | tf_op jit(solution)/shard_map/ppermute | solution.py:53
  21.5 3.9 %collective-permute-done.6 = bf16[32,3584]{1,0:T(8,128)(2,1)S(1)} collective-permute-done((bf16[32,3584]{1,0:T(8,128)(2,1)S(1)}, bf16[32,3584]{1,0:T(8,128)(2,1)S(1)}, u32[]{:S(2)}, u32[]{:S(2)}) %collective-permute-start.6) | collective-permute-done | bytes 229408 | tf_op jit(solution)/shard_map/ppermute | solution.py:53
  25.5 1.6 %collective-permute-start.7 = (bf16[64,3584]{1,0:T(8,128)(2,1)S(1)}, bf16[64,3584]{1,0:T(8,128)(2,1)S(1)}, u32[]{:S(2)}, u32[]{:S(2)}) collective-permute-start(bf16[64,3584]{1,0:T(8,128)(2,1)S(1)} %pad_maximum_fusion.3), channel_id=1, source_target_pairs={{0,4},{1,3},{2,6},{3,1},{4,0},{5,7},{6,2},{7,5},{8,12},{9,11},{10,... | collective-permute-start | bytes 1376264 | tf_op jit(solution)/shard_map/ppermute | solution.py:53
  27.1 6.6 %collective-permute-done.3 = bf16[64,3584]{1,0:T(8,128)(2,1)S(1)} collective-permute-done((bf16[64,3584]{1,0:T(8,128)(2,1)S(1)}, bf16[64,3584]{1,0:T(8,128)(2,1)S(1)}, u32[]{:S(2)}, u32[]{:S(2)}) %collective-permute-start.3) | collective-permute-done | bytes 458784 | tf_op jit(solution)/shard_map/ppermute | solution.py:53
  40.4 2.2 %collective-permute-start.13 = (f32[3,8,64]{2,1,0:T(8,128)S(1)}, f32[3,8,64]{2,1,0:T(8,128)S(1)}, u32[]{:S(2)}, u32[]{:S(2)}) collective-permute-start(f32[3,8,64]{2,1,0:T(8,128)S(1)} %add_select_fusion.2), channel_id=1, source_target_pairs={{0,6},{1,7},{2,4},{3,5},{4,2},{5,3},{6,0},{7,1},{8,14},{9,15},{10,... | collective-permute-start | bytes 18440 | tf_op jit(solution)/shard_map/ppermute | solution.py:212
  46.9 2.8 %collective-permute-start.16 = (f32[3,8,64]{2,1,0:T(8,128)S(1)}, f32[3,8,64]{2,1,0:T(8,128)S(1)}, u32[]{:S(2)}, u32[]{:S(2)}) collective-permute-start(f32[3,8,64]{2,1,0:T(8,128)S(1)} %add_select_fusion.1), channel_id=1, source_target_pairs={{0,24},{1,25},{2,26},{3,27},{4,28},{5,29},{6,30},{7,31},{8,16},{9,... | collective-permute-start | bytes 18440 | tf_op jit(solution)/shard_map/ppermute | solution.py:212
  49.7 1.6 %collective-permute-start.14 = (f32[3,8,64]{2,1,0:T(8,128)S(1)}, f32[3,8,64]{2,1,0:T(8,128)S(1)}, u32[]{:S(2)}, u32[]{:S(2)}) collective-permute-start(f32[3,8,64]{2,1,0:T(8,128)S(1)} %add_select_fusion.1), channel_id=1, source_target_pairs={{0,8},{1,9},{2,10},{3,11},{4,12},{5,13},{6,14},{7,15},{8,0},{9,1},... | collective-permute-start | bytes 18440 | tf_op jit(solution)/shard_map/ppermute | solution.py:212
  52.5 1.8 %collective-permute-done.15 = f32[3,8,64]{2,1,0:T(8,128)S(1)} collective-permute-done((f32[3,8,64]{2,1,0:T(8,128)S(1)}, f32[3,8,64]{2,1,0:T(8,128)S(1)}, u32[]{:S(2)}, u32[]{:S(2)}) %collective-permute-start.15) | collective-permute-done | bytes 6176 | tf_op jit(solution)/shard_map/ppermute | solution.py:212
  54.9 1.6 %convolution_convert_fusion.1 = bf16[256,3584]{1,0:T(8,128)(2,1)S(1)} fusion(bf16[256,768]{1,0:T(8,128)(2,1)S(1)} %get-tuple-element.11, bf16[3584,768]{1,0:T(8,128)(2,1)S(1)} %copy-done.1), kind=kOutput, calls=%fused_computation.1 | convolution fusion | flops 1410203648 | bytes 7733248 | tf_op jit(solution)/shard_map/dot_general | solution.py:219
  56.5 1.6 %fusion.19 = f32[256,3584]{1,0:T(8,128)S(1)} fusion(bf16[256,768]{1,0:T(8,128)(2,1)S(1)} %get-tuple-element.13, bf16[3584,768]{1,0:T(8,128)(2,1)S(1)} %copy-done.1), kind=kOutput, calls=%fused_computation.46 | convolution fusion | flops 1409286144 | bytes 9568256 | tf_op jit(solution)/shard_map/dot_general | solution.py:219
  59.8 4.8 %convolution_convert_fusion = bf16[3584,768]{1,0:T(8,128)(2,1)} fusion(bf16[128,3584]{1,0:T(8,128)(2,1)S(1)} %collective-permute-done.9, bf16[128,3584]{1,0:T(8,128)(2,1)S(1)} %collective-permute-done.8, bf16[128,3584]{1,0:T(8,128)(2,1)S(1)} %pad_maximum_fusion.1, bf16[128,3584]{1,0:T(8,128)(2,1)S(1)} %pad_maximum_fusion, ...), kind=kOutput, calls=%fused_computation | convolution fusion | flops 2837577728 | bytes 9961472 | tf_op jit(solution)/shard_map/dot_general | solution.py:219
  67.7 10.5 %collective-permute-done.23 = bf16[64,3584]{1,0:T(8,128)(2,1)S(1)} collective-permute-done((bf16[64,3584]{1,0:T(8,128)(2,1)S(1)}, bf16[64,3584]{1,0:T(8,128)(2,1)S(1)}, u32[]{:S(2)}, u32[]{:S(2)}) %collective-permute-start.23) | collective-permute-done | bytes 458784 | tf_op jit(solution)/shard_map/ppermute | solution.py:53
  79.2 1.6 %collective-permute-start.19 = (bf16[32,3584]{1,0:T(8,128)(2,1)S(1)}, bf16[32,3584]{1,0:T(8,128)(2,1)S(1)}, u32[]{:S(2)}, u32[]{:S(2)}) collective-permute-start(bf16[32,3584]{1,0:T(8,128)(2,1)S(1)} %slice.93), channel_id=1, source_target_pairs={{0,4},{1,3},{2,6},{3,1},{4,0},{5,7},{6,2},{7,5},{8,12},{9,11},{10,... | collective-permute-start | bytes 688136 | tf_op jit(solution)/shard_map/ppermute | solution.py:53
  80.8 5.1 %collective-permute-done.24 = bf16[32,3584]{1,0:T(8,128)(2,1)S(1)} collective-permute-done((bf16[32,3584]{1,0:T(8,128)(2,1)S(1)}, bf16[32,3584]{1,0:T(8,128)(2,1)S(1)}, u32[]{:S(2)}, u32[]{:S(2)}) %collective-permute-start.24) | collective-permute-done | bytes 229408 | tf_op jit(solution)/shard_map/ppermute | solution.py:53
  88.0 2.8 %collective-permute-done.25 = bf16[16,3584]{1,0:T(8,128)(2,1)S(1)} collective-permute-done((bf16[16,3584]{1,0:T(8,128)(2,1)S(1)}, bf16[16,3584]{1,0:T(8,128)(2,1)S(1)}, u32[]{:S(2)}, u32[]{:S(2)}) %collective-permute-start.25) | collective-permute-done | bytes 114720 | tf_op jit(solution)/shard_map/ppermute | solution.py:53
  92.0 2.0 %collective-permute-start.21 = (bf16[8,3584]{1,0:T(8,128)(2,1)S(1)}, bf16[8,3584]{1,0:T(8,128)(2,1)S(1)}, u32[]{:S(2)}, u32[]{:S(2)}) collective-permute-start(bf16[8,3584]{1,0:T(8,128)(2,1)S(1)} %slice.97), channel_id=1, source_target_pairs={{0,16},{1,9},{2,18},{3,11},{4,20},{5,13},{6,22},{7,15},{8,24},{9,1... | collective-permute-start | bytes 172040 | tf_op jit(solution)/shard_map/ppermute | solution.py:53
  94.0 2.0 %collective-permute-done.26 = bf16[8,3584]{1,0:T(8,128)(2,1)S(1)} collective-permute-done((bf16[8,3584]{1,0:T(8,128)(2,1)S(1)}, bf16[8,3584]{1,0:T(8,128)(2,1)S(1)}, u32[]{:S(2)}, u32[]{:S(2)}) %collective-permute-start.26) | collective-permute-done | bytes 57376 | tf_op jit(solution)/shard_map/ppermute | solution.py:53
  96.1 1.7 %collective-permute-done.21 = bf16[8,3584]{1,0:T(8,128)(2,1)S(1)} collective-permute-done((bf16[8,3584]{1,0:T(8,128)(2,1)S(1)}, bf16[8,3584]{1,0:T(8,128)(2,1)S(1)}, u32[]{:S(2)}, u32[]{:S(2)}) %collective-permute-start.21) | collective-permute-done | bytes 57376 | tf_op jit(solution)/shard_map/ppermute | solution.py:53
  (78 shorter events, 25.5 us)
Async XLA Ops:
  1.5 6.4 %collective-permute-start = (bf16[8,3584]{1,0:T(8,128)(2,1)S(1)}, bf16[8,3584]{1,0:T(8,128)(2,1)S(1)}, u32[]{:S(2)}, u32[]{:S(2)}) collective-permute-start(bf16[8,3584]{1,0:T(8,128)(2,1)S(1)} %get-tuple-element.22), channel_id=1, source_target_pairs={{0,16},{1,9},{2,18},{3,11},{4,20},{5,13},{6,22},{7,15},{8,24},{9,1... | collective-permute-start | bytes 172040 | tf_op jit(solution)/shard_map/ppermute | solution.py:53
  5.6 7.6 %collective-permute-start.4 = (bf16[8,3584]{1,0:T(8,128)(2,1)S(1)}, bf16[8,3584]{1,0:T(8,128)(2,1)S(1)}, u32[]{:S(2)}, u32[]{:S(2)}) collective-permute-start(bf16[8,3584]{1,0:T(8,128)(2,1)S(1)} %get-tuple-element.21), channel_id=1, source_target_pairs={{0,16},{1,9},{2,18},{3,11},{4,20},{5,13},{6,22},{7,15},{8,24},{9,1... | collective-permute-start | bytes 172040 | tf_op jit(solution)/shard_map/ppermute | solution.py:53
  7.9 6.9 %collective-permute-start.1 = (bf16[16,3584]{1,0:T(8,128)(2,1)S(1)}, bf16[16,3584]{1,0:T(8,128)(2,1)S(1)}, u32[]{:S(2)}, u32[]{:S(2)}) collective-permute-start(bf16[16,3584]{1,0:T(8,128)(2,1)S(1)} %pad_maximum_fusion.6), channel_id=1, source_target_pairs={{0,8},{1,17},{2,10},{3,19},{4,12},{5,21},{6,14},{7,23},{8,0},{9,25... | collective-permute-start | bytes 344072 | tf_op jit(solution)/shard_map/ppermute | solution.py:53
  13.2 6.1 %collective-permute-start.5 = (bf16[16,3584]{1,0:T(8,128)(2,1)S(1)}, bf16[16,3584]{1,0:T(8,128)(2,1)S(1)}, u32[]{:S(2)}, u32[]{:S(2)}) collective-permute-start(bf16[16,3584]{1,0:T(8,128)(2,1)S(1)} %pad_maximum_fusion.7), channel_id=1, source_target_pairs={{0,2},{1,5},{2,0},{3,7},{4,6},{5,1},{6,4},{7,3},{8,10},{9,13},{10,... | collective-permute-start | bytes 344072 | tf_op jit(solution)/shard_map/ppermute | solution.py:53
  14.8 6.1 %collective-permute-start.2 = (bf16[32,3584]{1,0:T(8,128)(2,1)S(1)}, bf16[32,3584]{1,0:T(8,128)(2,1)S(1)}, u32[]{:S(2)}, u32[]{:S(2)}) collective-permute-start(bf16[32,3584]{1,0:T(8,128)(2,1)S(1)} %pad_maximum_fusion.4), channel_id=1, source_target_pairs={{0,4},{1,3},{2,6},{3,1},{4,0},{5,7},{6,2},{7,5},{8,12},{9,11},{10,... | collective-permute-start | bytes 688136 | tf_op jit(solution)/shard_map/ppermute | solution.py:53
  19.3 6.1 %collective-permute-start.6 = (bf16[32,3584]{1,0:T(8,128)(2,1)S(1)}, bf16[32,3584]{1,0:T(8,128)(2,1)S(1)}, u32[]{:S(2)}, u32[]{:S(2)}) collective-permute-start(bf16[32,3584]{1,0:T(8,128)(2,1)S(1)} %pad_maximum_fusion.5), channel_id=1, source_target_pairs={{0,8},{1,17},{2,10},{3,19},{4,12},{5,21},{6,14},{7,23},{8,0},{9,25... | collective-permute-start | bytes 688136 | tf_op jit(solution)/shard_map/ppermute | solution.py:53
  21.0 12.7 %collective-permute-start.3 = (bf16[64,3584]{1,0:T(8,128)(2,1)S(1)}, bf16[64,3584]{1,0:T(8,128)(2,1)S(1)}, u32[]{:S(2)}, u32[]{:S(2)}) collective-permute-start(bf16[64,3584]{1,0:T(8,128)(2,1)S(1)} %pad_maximum_fusion.2), channel_id=1, source_target_pairs={{0,2},{1,5},{2,0},{3,7},{4,6},{5,1},{6,4},{7,3},{8,10},{9,13},{10,... | collective-permute-start | bytes 1376264 | tf_op jit(solution)/shard_map/ppermute | solution.py:53
  25.5 8.5 %collective-permute-start.7 = (bf16[64,3584]{1,0:T(8,128)(2,1)S(1)}, bf16[64,3584]{1,0:T(8,128)(2,1)S(1)}, u32[]{:S(2)}, u32[]{:S(2)}) collective-permute-start(bf16[64,3584]{1,0:T(8,128)(2,1)S(1)} %pad_maximum_fusion.3), channel_id=1, source_target_pairs={{0,4},{1,3},{2,6},{3,1},{4,0},{5,7},{6,2},{7,5},{8,12},{9,11},{10,... | collective-permute-start | bytes 1376264 | tf_op jit(solution)/shard_map/ppermute | solution.py:53
  40.4 4.6 %collective-permute-start.13 = (f32[3,8,64]{2,1,0:T(8,128)S(1)}, f32[3,8,64]{2,1,0:T(8,128)S(1)}, u32[]{:S(2)}, u32[]{:S(2)}) collective-permute-start(f32[3,8,64]{2,1,0:T(8,128)S(1)} %add_select_fusion.2), channel_id=1, source_target_pairs={{0,6},{1,7},{2,4},{3,5},{4,2},{5,3},{6,0},{7,1},{8,14},{9,15},{10,... | collective-permute-start | bytes 18440 | tf_op jit(solution)/shard_map/ppermute | solution.py:212
  42.6 3.7 %collective-permute-start.12 = (f32[3,8,64]{2,1,0:T(8,128)S(1)}, f32[3,8,64]{2,1,0:T(8,128)S(1)}, u32[]{:S(2)}, u32[]{:S(2)}) collective-permute-start(f32[3,8,64]{2,1,0:T(8,128)S(1)} %add_select_fusion.2), channel_id=1, source_target_pairs={{0,4},{1,5},{2,6},{3,7},{4,0},{5,1},{6,2},{7,3},{8,12},{9,13},{10,... | collective-permute-start | bytes 18440 | tf_op jit(solution)/shard_map/ppermute | solution.py:212
  43.1 3.7 %collective-permute-start.11 = (f32[3,8,64]{2,1,0:T(8,128)S(1)}, f32[3,8,64]{2,1,0:T(8,128)S(1)}, u32[]{:S(2)}, u32[]{:S(2)}) collective-permute-start(f32[3,8,64]{2,1,0:T(8,128)S(1)} %add_select_fusion.2), channel_id=1, source_target_pairs={{0,2},{1,3},{2,0},{3,1},{4,6},{5,7},{6,4},{7,5},{8,10},{9,11},{10,... | collective-permute-start | bytes 18440 | tf_op jit(solution)/shard_map/ppermute | solution.py:212
  46.9 5.6 %collective-permute-start.16 = (f32[3,8,64]{2,1,0:T(8,128)S(1)}, f32[3,8,64]{2,1,0:T(8,128)S(1)}, u32[]{:S(2)}, u32[]{:S(2)}) collective-permute-start(f32[3,8,64]{2,1,0:T(8,128)S(1)} %add_select_fusion.1), channel_id=1, source_target_pairs={{0,24},{1,25},{2,26},{3,27},{4,28},{5,29},{6,30},{7,31},{8,16},{9,... | collective-permute-start | bytes 18440 | tf_op jit(solution)/shard_map/ppermute | solution.py:212
  49.7 4.6 %collective-permute-start.15 = (f32[3,8,64]{2,1,0:T(8,128)S(1)}, f32[3,8,64]{2,1,0:T(8,128)S(1)}, u32[]{:S(2)}, u32[]{:S(2)}) collective-permute-start(f32[3,8,64]{2,1,0:T(8,128)S(1)} %add_select_fusion.1), channel_id=1, source_target_pairs={{0,16},{1,17},{2,18},{3,19},{4,20},{5,21},{6,22},{7,23},{8,24},{9,... | collective-permute-start | bytes 18440 | tf_op jit(solution)/shard_map/ppermute | solution.py:212
  49.7 4.6 %collective-permute-start.14 = (f32[3,8,64]{2,1,0:T(8,128)S(1)}, f32[3,8,64]{2,1,0:T(8,128)S(1)}, u32[]{:S(2)}, u32[]{:S(2)}) collective-permute-start(f32[3,8,64]{2,1,0:T(8,128)S(1)} %add_select_fusion.1), channel_id=1, source_target_pairs={{0,8},{1,9},{2,10},{3,11},{4,12},{5,13},{6,14},{7,15},{8,0},{9,1},... | collective-permute-start | bytes 18440 | tf_op jit(solution)/shard_map/ppermute | solution.py:212
  58.3 6.3 %collective-permute-start.22 = (bf16[128,3584]{1,0:T(8,128)(2,1)S(1)}, bf16[128,3584]{1,0:T(8,128)(2,1)S(1)}, u32[]{:S(2)}, u32[]{:S(2)}) collective-permute-start(bf16[128,3584]{1,0:T(8,128)(2,1)S(1)} %get-tuple-element.20), channel_id=1, source_target_pairs={{0,1},{1,0},{2,3},{3,2},{4,5},{5,4},{6,7},{7,6},{8,9},{9,8},{10,11... | collective-permute-start | bytes 2752520 | tf_op jit(solution)/shard_map/ppermute | solution.py:57
  59.3 6.9 %collective-permute-start.17 = (bf16[128,3584]{1,0:T(8,128)(2,1)S(1)}, bf16[128,3584]{1,0:T(8,128)(2,1)S(1)}, u32[]{:S(2)}, u32[]{:S(2)}) collective-permute-start(bf16[128,3584]{1,0:T(8,128)(2,1)S(1)} %get-tuple-element.19), channel_id=1, source_target_pairs={{0,1},{1,0},{2,3},{3,2},{4,5},{5,4},{6,7},{7,6},{8,9},{9,8},{10,11... | collective-permute-start | bytes 2752520 | tf_op jit(solution)/shard_map/ppermute | solution.py:57
  64.8 13.4 %collective-permute-start.23 = (bf16[64,3584]{1,0:T(8,128)(2,1)S(1)}, bf16[64,3584]{1,0:T(8,128)(2,1)S(1)}, u32[]{:S(2)}, u32[]{:S(2)}) collective-permute-start(bf16[64,3584]{1,0:T(8,128)(2,1)S(1)} %slice.99), channel_id=1, source_target_pairs={{0,4},{1,3},{2,6},{3,1},{4,0},{5,7},{6,2},{7,5},{8,12},{9,11},{10,... | collective-permute-start | bytes 1376264 | tf_op jit(solution)/shard_map/ppermute | solution.py:53
  66.4 12.7 %collective-permute-start.18 = (bf16[64,3584]{1,0:T(8,128)(2,1)S(1)}, bf16[64,3584]{1,0:T(8,128)(2,1)S(1)}, u32[]{:S(2)}, u32[]{:S(2)}) collective-permute-start(bf16[64,3584]{1,0:T(8,128)(2,1)S(1)} %slice.91), channel_id=1, source_target_pairs={{0,2},{1,5},{2,0},{3,7},{4,6},{5,1},{6,4},{7,3},{8,10},{9,13},{10,... | collective-permute-start | bytes 1376264 | tf_op jit(solution)/shard_map/ppermute | solution.py:53
  78.3 7.6 %collective-permute-start.24 = (bf16[32,3584]{1,0:T(8,128)(2,1)S(1)}, bf16[32,3584]{1,0:T(8,128)(2,1)S(1)}, u32[]{:S(2)}, u32[]{:S(2)}) collective-permute-start(bf16[32,3584]{1,0:T(8,128)(2,1)S(1)} %slice.101), channel_id=1, source_target_pairs={{0,8},{1,17},{2,10},{3,19},{4,12},{5,21},{6,14},{7,23},{8,0},{9,25... | collective-permute-start | bytes 688136 | tf_op jit(solution)/shard_map/ppermute | solution.py:53
  79.2 7.7 %collective-permute-start.19 = (bf16[32,3584]{1,0:T(8,128)(2,1)S(1)}, bf16[32,3584]{1,0:T(8,128)(2,1)S(1)}, u32[]{:S(2)}, u32[]{:S(2)}) collective-permute-start(bf16[32,3584]{1,0:T(8,128)(2,1)S(1)} %slice.93), channel_id=1, source_target_pairs={{0,4},{1,3},{2,6},{3,1},{4,0},{5,7},{6,2},{7,5},{8,12},{9,11},{10,... | collective-permute-start | bytes 688136 | tf_op jit(solution)/shard_map/ppermute | solution.py:53
  86.0 4.9 %collective-permute-start.25 = (bf16[16,3584]{1,0:T(8,128)(2,1)S(1)}, bf16[16,3584]{1,0:T(8,128)(2,1)S(1)}, u32[]{:S(2)}, u32[]{:S(2)}) collective-permute-start(bf16[16,3584]{1,0:T(8,128)(2,1)S(1)} %slice.103), channel_id=1, source_target_pairs={{0,2},{1,5},{2,0},{3,7},{4,6},{5,1},{6,4},{7,3},{8,10},{9,13},{10,... | collective-permute-start | bytes 344072 | tf_op jit(solution)/shard_map/ppermute | solution.py:53
  87.0 5.0 %collective-permute-start.20 = (bf16[16,3584]{1,0:T(8,128)(2,1)S(1)}, bf16[16,3584]{1,0:T(8,128)(2,1)S(1)}, u32[]{:S(2)}, u32[]{:S(2)}) collective-permute-start(bf16[16,3584]{1,0:T(8,128)(2,1)S(1)} %slice.95), channel_id=1, source_target_pairs={{0,8},{1,17},{2,10},{3,19},{4,12},{5,21},{6,14},{7,23},{8,0},{9,25... | collective-permute-start | bytes 344072 | tf_op jit(solution)/shard_map/ppermute | solution.py:53
  90.9 5.1 %collective-permute-start.26 = (bf16[8,3584]{1,0:T(8,128)(2,1)S(1)}, bf16[8,3584]{1,0:T(8,128)(2,1)S(1)}, u32[]{:S(2)}, u32[]{:S(2)}) collective-permute-start(bf16[8,3584]{1,0:T(8,128)(2,1)S(1)} %slice.105), channel_id=1, source_target_pairs={{0,16},{1,9},{2,18},{3,11},{4,20},{5,13},{6,22},{7,15},{8,24},{9,1... | collective-permute-start | bytes 172040 | tf_op jit(solution)/shard_map/ppermute | solution.py:53
  92.0 5.8 %collective-permute-start.21 = (bf16[8,3584]{1,0:T(8,128)(2,1)S(1)}, bf16[8,3584]{1,0:T(8,128)(2,1)S(1)}, u32[]{:S(2)}, u32[]{:S(2)}) collective-permute-start(bf16[8,3584]{1,0:T(8,128)(2,1)S(1)} %slice.97), channel_id=1, source_target_pairs={{0,16},{1,9},{2,18},{3,11},{4,20},{5,13},{6,22},{7,15},{8,24},{9,1... | collective-permute-start | bytes 172040 | tf_op jit(solution)/shard_map/ppermute | solution.py:53
  (5 other events, 37.3 us)

commit v3 on v2

--- a/solution.py
+++ b/solution.py
@@ -10,7 +10,7 @@
 AXIS = "vocab"
 ROW_TILE = 8
 STATS_RADIX_BITS = 2
-VMEM_BYTES = 12 << 20
+VMEM_BYTES = 2 << 20
 
 
 def stage_orders(size, groups):
@@ -23,8 +23,8 @@
         for start in range(0, len(bits), 2):
             pair = bits[start : start + 2]
             turn = odd and start > 0
-            low += pair[::-1] if turn else pair
-            high += pair if turn else pair[::-1]
+            low += pair if turn else pair[::-1]
+            high += pair[::-1] if turn else pair
         if odd and half:
             for order in (low, high):
                 order[half - 1], order[half] = order[half], order[half - 1]

time: 98.6 us -> 99.6 us (1.010)
    ppermute x16, waiting for transfers between devices: 43 us -> 45.1 us  [swap(): return lax.ppermute(value, AXIS, pairs)]
  transfers between devices with their start and end apart: 27 -> 27, of which waited for: 21 -> 20; matrix products, arithmetic and copies ran while one was open for 9% -> 9% of each run, Pallas kernels for 1% -> 1%
where the time goes in v3:
time: 99.6 us; the launch traced here: 99.4 us
  waiting for transfers between devices  50.8 us (51%)
  starting transfers between devices  30.8 us (31%)
  matrix products  11.6 us (12%)
  other arithmetic  1.9 us (2%)
  Pallas kernels  1.77 us (2%)
  local copies, waits for them, and re-layouts  1.58 us (2%)
    ppermute x16, waiting for transfers between devices, swap(): return lax.ppermute(value, AXIS, pairs)  45.1 us
    ppermute x16, starting transfers between devices, swap(): return lax.ppermute(value, AXIS, pairs)  21.6 us
    dot_general x7, matrix products, matmul(): lax.dot_general(left, right, (contract, ((), ())), preferred_element_type...  11.6 us
    ppermute x6, starting transfers between devices, exchange_stats(): lax.ppermute(stats, AXIS, [(i, i ^ mask) for i in range(size)])  7.96 us
    ppermute x6, waiting for transfers between devices, exchange_stats(): lax.ppermute(stats, AXIS, [(i, i ^ mask) for i in range(size)])  4.89 us
  transfers between devices with their start and end apart: 27, of which 20 were waited for; matrix products, arithmetic and copies ran while one was open for 9% of the time, Pallas kernels for 1%

profile of v3, /device:TPU:0, one launch (start us, length us, event | category | flops | bytes accessed | tf_op | source)
XLA Modules:
  0.0 99.4 jit_solution(6000263079292743961)
XLA Ops:
  1.5 3.1 %collective-permute-start = (bf16[8,3584]{1,0:T(8,128)(2,1)S(1)}, bf16[8,3584]{1,0:T(8,128)(2,1)S(1)}, u32[]{:S(2)}, u32[]{:S(2)}) collective-permute-start(bf16[8,3584]{1,0:T(8,128)(2,1)S(1)} %get-tuple-element.22), channel_id=1, source_target_pairs={{0,8},{1,17},{2,10},{3,19},{4,12},{5,21},{6,14},{7,23},{8,0},{9,25... | collective-permute-start | bytes 172040 | tf_op jit(solution)/shard_map/ppermute | solution.py:53
  4.7 2.7 %collective-permute-done = bf16[8,3584]{1,0:T(8,128)(2,1)S(1)} collective-permute-done((bf16[8,3584]{1,0:T(8,128)(2,1)S(1)}, bf16[8,3584]{1,0:T(8,128)(2,1)S(1)}, u32[]{:S(2)}, u32[]{:S(2)}) %collective-permute-start) | collective-permute-done | bytes 57376 | tf_op jit(solution)/shard_map/ppermute | solution.py:53
  7.4 2.5 %collective-permute-start.1 = (bf16[16,3584]{1,0:T(8,128)(2,1)S(1)}, bf16[16,3584]{1,0:T(8,128)(2,1)S(1)}, u32[]{:S(2)}, u32[]{:S(2)}) collective-permute-start(bf16[16,3584]{1,0:T(8,128)(2,1)S(1)} %pad_maximum_fusion.6), channel_id=1, source_target_pairs={{0,16},{1,9},{2,18},{3,11},{4,20},{5,13},{6,22},{7,15},{8,24},{9,1... | collective-permute-start | bytes 344072 | tf_op jit(solution)/shard_map/ppermute | solution.py:53
  9.9 1.6 %collective-permute-start.5 = (bf16[16,3584]{1,0:T(8,128)(2,1)S(1)}, bf16[16,3584]{1,0:T(8,128)(2,1)S(1)}, u32[]{:S(2)}, u32[]{:S(2)}) collective-permute-start(bf16[16,3584]{1,0:T(8,128)(2,1)S(1)} %pad_maximum_fusion.7), channel_id=1, source_target_pairs={{0,4},{1,3},{2,6},{3,1},{4,0},{5,7},{6,2},{7,5},{8,12},{9,11},{10,... | collective-permute-start | bytes 344072 | tf_op jit(solution)/shard_map/ppermute | solution.py:53
  11.5 1.7 %collective-permute-done.1 = bf16[16,3584]{1,0:T(8,128)(2,1)S(1)} collective-permute-done((bf16[16,3584]{1,0:T(8,128)(2,1)S(1)}, bf16[16,3584]{1,0:T(8,128)(2,1)S(1)}, u32[]{:S(2)}, u32[]{:S(2)}) %collective-permute-start.1) | collective-permute-done | bytes 114720 | tf_op jit(solution)/shard_map/ppermute | solution.py:53
  13.2 1.8 %collective-permute-start.2 = (bf16[32,3584]{1,0:T(8,128)(2,1)S(1)}, bf16[32,3584]{1,0:T(8,128)(2,1)S(1)}, u32[]{:S(2)}, u32[]{:S(2)}) collective-permute-start(bf16[32,3584]{1,0:T(8,128)(2,1)S(1)} %pad_maximum_fusion.4), channel_id=1, source_target_pairs={{0,2},{1,5},{2,0},{3,7},{4,6},{5,1},{6,4},{7,3},{8,10},{9,13},{10,... | collective-permute-start | bytes 688136 | tf_op jit(solution)/shard_map/ppermute | solution.py:53
  17.3 2.0 %collective-permute-done.2 = bf16[32,3584]{1,0:T(8,128)(2,1)S(1)} collective-permute-done((bf16[32,3584]{1,0:T(8,128)(2,1)S(1)}, bf16[32,3584]{1,0:T(8,128)(2,1)S(1)}, u32[]{:S(2)}, u32[]{:S(2)}) %collective-permute-start.2) | collective-permute-done | bytes 229408 | tf_op jit(solution)/shard_map/ppermute | solution.py:53
  19.3 1.8 %collective-permute-start.3 = (bf16[64,3584]{1,0:T(8,128)(2,1)S(1)}, bf16[64,3584]{1,0:T(8,128)(2,1)S(1)}, u32[]{:S(2)}, u32[]{:S(2)}) collective-permute-start(bf16[64,3584]{1,0:T(8,128)(2,1)S(1)} %pad_maximum_fusion.2), channel_id=1, source_target_pairs={{0,4},{1,3},{2,6},{3,1},{4,0},{5,7},{6,2},{7,5},{8,12},{9,11},{10,... | collective-permute-start | bytes 1376264 | tf_op jit(solution)/shard_map/ppermute | solution.py:53
  21.1 4.3 %collective-permute-done.6 = bf16[32,3584]{1,0:T(8,128)(2,1)S(1)} collective-permute-done((bf16[32,3584]{1,0:T(8,128)(2,1)S(1)}, bf16[32,3584]{1,0:T(8,128)(2,1)S(1)}, u32[]{:S(2)}, u32[]{:S(2)}) %collective-permute-start.6) | collective-permute-done | bytes 229408 | tf_op jit(solution)/shard_map/ppermute | solution.py:53
  27.0 4.0 %collective-permute-done.3 = bf16[64,3584]{1,0:T(8,128)(2,1)S(1)} collective-permute-done((bf16[64,3584]{1,0:T(8,128)(2,1)S(1)}, bf16[64,3584]{1,0:T(8,128)(2,1)S(1)}, u32[]{:S(2)}, u32[]{:S(2)}) %collective-permute-start.3) | collective-permute-done | bytes 458784 | tf_op jit(solution)/shard_map/ppermute | solution.py:53
  31.1 2.9 %collective-permute-done.7 = bf16[64,3584]{1,0:T(8,128)(2,1)S(1)} collective-permute-done((bf16[64,3584]{1,0:T(8,128)(2,1)S(1)}, bf16[64,3584]{1,0:T(8,128)(2,1)S(1)}, u32[]{:S(2)}, u32[]{:S(2)}) %collective-permute-start.7) | collective-permute-done | bytes 458784 | tf_op jit(solution)/shard_map/ppermute | solution.py:53
  40.1 2.5 %collective-permute-start.13 = (f32[3,8,64]{2,1,0:T(8,128)S(1)}, f32[3,8,64]{2,1,0:T(8,128)S(1)}, u32[]{:S(2)}, u32[]{:S(2)}) collective-permute-start(f32[3,8,64]{2,1,0:T(8,128)S(1)} %add_select_fusion.2), channel_id=1, source_target_pairs={{0,6},{1,7},{2,4},{3,5},{4,2},{5,3},{6,0},{7,1},{8,14},{9,15},{10,... | collective-permute-start | bytes 18440 | tf_op jit(solution)/shard_map/ppermute | solution.py:212
  48.4 3.0 %collective-permute-start.14 = (f32[3,8,64]{2,1,0:T(8,128)S(1)}, f32[3,8,64]{2,1,0:T(8,128)S(1)}, u32[]{:S(2)}, u32[]{:S(2)}) collective-permute-start(f32[3,8,64]{2,1,0:T(8,128)S(1)} %add_select_fusion.1), channel_id=1, source_target_pairs={{0,8},{1,9},{2,10},{3,11},{4,12},{5,13},{6,14},{7,15},{8,0},{9,1},... | collective-permute-start | bytes 18440 | tf_op jit(solution)/shard_map/ppermute | solution.py:212
  53.6 1.6 %convolution_convert_fusion.1 = bf16[256,3584]{1,0:T(8,128)(2,1)S(1)} fusion(bf16[256,768]{1,0:T(8,128)(2,1)S(1)} %get-tuple-element.11, bf16[3584,768]{1,0:T(8,128)(2,1)S(1)} %copy-done.1), kind=kOutput, calls=%fused_computation.1 | convolution fusion | flops 1410203648 | bytes 7733248 | tf_op jit(solution)/shard_map/dot_general | solution.py:219
  55.3 1.6 %fusion.19 = f32[256,3584]{1,0:T(8,128)S(1)} fusion(bf16[256,768]{1,0:T(8,128)(2,1)S(1)} %get-tuple-element.13, bf16[3584,768]{1,0:T(8,128)(2,1)S(1)} %copy-done.1), kind=kOutput, calls=%fused_computation.46 | convolution fusion | flops 1409286144 | bytes 9568256 | tf_op jit(solution)/shard_map/dot_general | solution.py:219
  58.6 4.8 %convolution_convert_fusion = bf16[3584,768]{1,0:T(8,128)(2,1)} fusion(bf16[128,3584]{1,0:T(8,128)(2,1)S(1)} %collective-permute-done.9, bf16[128,3584]{1,0:T(8,128)(2,1)S(1)} %collective-permute-done.8, bf16[128,3584]{1,0:T(8,128)(2,1)S(1)} %pad_maximum_fusion.1, bf16[128,3584]{1,0:T(8,128)(2,1)S(1)} %pad_maximum_fusion, ...), kind=kOutput, calls=%fused_computation | convolution fusion | flops 2837577728 | bytes 9961472 | tf_op jit(solution)/shard_map/dot_general | solution.py:219
  65.0 1.6 %collective-permute-start.18 = (bf16[64,3584]{1,0:T(8,128)(2,1)S(1)}, bf16[64,3584]{1,0:T(8,128)(2,1)S(1)}, u32[]{:S(2)}, u32[]{:S(2)}) collective-permute-start(bf16[64,3584]{1,0:T(8,128)(2,1)S(1)} %slice.91), channel_id=1, source_target_pairs={{0,4},{1,3},{2,6},{3,1},{4,0},{5,7},{6,2},{7,5},{8,12},{9,11},{10,... | collective-permute-start | bytes 1376264 | tf_op jit(solution)/shard_map/ppermute | solution.py:53
  66.6 10.0 %collective-permute-done.23 = bf16[64,3584]{1,0:T(8,128)(2,1)S(1)} collective-permute-done((bf16[64,3584]{1,0:T(8,128)(2,1)S(1)}, bf16[64,3584]{1,0:T(8,128)(2,1)S(1)}, u32[]{:S(2)}, u32[]{:S(2)}) %collective-permute-start.23) | collective-permute-done | bytes 458784 | tf_op jit(solution)/shard_map/ppermute | solution.py:53
  76.7 2.0 %collective-permute-start.24 = (bf16[32,3584]{1,0:T(8,128)(2,1)S(1)}, bf16[32,3584]{1,0:T(8,128)(2,1)S(1)}, u32[]{:S(2)}, u32[]{:S(2)}) collective-permute-start(bf16[32,3584]{1,0:T(8,128)(2,1)S(1)} %slice.101), channel_id=1, source_target_pairs={{0,16},{1,9},{2,18},{3,11},{4,20},{5,13},{6,22},{7,15},{8,24},{9,1... | collective-permute-start | bytes 688136 | tf_op jit(solution)/shard_map/ppermute | solution.py:53
  80.1 6.2 %collective-permute-done.24 = bf16[32,3584]{1,0:T(8,128)(2,1)S(1)} collective-permute-done((bf16[32,3584]{1,0:T(8,128)(2,1)S(1)}, bf16[32,3584]{1,0:T(8,128)(2,1)S(1)}, u32[]{:S(2)}, u32[]{:S(2)}) %collective-permute-start.24) | collective-permute-done | bytes 229408 | tf_op jit(solution)/shard_map/ppermute | solution.py:53
  86.3 1.6 %collective-permute-start.25 = (bf16[16,3584]{1,0:T(8,128)(2,1)S(1)}, bf16[16,3584]{1,0:T(8,128)(2,1)S(1)}, u32[]{:S(2)}, u32[]{:S(2)}) collective-permute-start(bf16[16,3584]{1,0:T(8,128)(2,1)S(1)} %slice.103), channel_id=1, source_target_pairs={{0,4},{1,3},{2,6},{3,1},{4,0},{5,7},{6,2},{7,5},{8,12},{9,11},{10,... | collective-permute-start | bytes 344072 | tf_op jit(solution)/shard_map/ppermute | solution.py:53
  88.1 3.1 %collective-permute-done.25 = bf16[16,3584]{1,0:T(8,128)(2,1)S(1)} collective-permute-done((bf16[16,3584]{1,0:T(8,128)(2,1)S(1)}, bf16[16,3584]{1,0:T(8,128)(2,1)S(1)}, u32[]{:S(2)}, u32[]{:S(2)}) %collective-permute-start.25) | collective-permute-done | bytes 114720 | tf_op jit(solution)/shard_map/ppermute | solution.py:53
  91.3 3.2 %collective-permute-done.20 = bf16[16,3584]{1,0:T(8,128)(2,1)S(1)} collective-permute-done((bf16[16,3584]{1,0:T(8,128)(2,1)S(1)}, bf16[16,3584]{1,0:T(8,128)(2,1)S(1)}, u32[]{:S(2)}, u32[]{:S(2)}) %collective-permute-start.20) | collective-permute-done | bytes 114720 | tf_op jit(solution)/shard_map/ppermute | solution.py:53
  95.5 3.3 %collective-permute-done.21 = bf16[8,3584]{1,0:T(8,128)(2,1)S(1)} collective-permute-done((bf16[8,3584]{1,0:T(8,128)(2,1)S(1)}, bf16[8,3584]{1,0:T(8,128)(2,1)S(1)}, u32[]{:S(2)}, u32[]{:S(2)}) %collective-permute-start.21) | collective-permute-done | bytes 57376 | tf_op jit(solution)/shard_map/ppermute | solution.py:53
  (78 shorter events, 25.8 us)
Async XLA Ops:
  1.5 5.9 %collective-permute-start = (bf16[8,3584]{1,0:T(8,128)(2,1)S(1)}, bf16[8,3584]{1,0:T(8,128)(2,1)S(1)}, u32[]{:S(2)}, u32[]{:S(2)}) collective-permute-start(bf16[8,3584]{1,0:T(8,128)(2,1)S(1)} %get-tuple-element.22), channel_id=1, source_target_pairs={{0,8},{1,17},{2,10},{3,19},{4,12},{5,21},{6,14},{7,23},{8,0},{9,25... | collective-permute-start | bytes 172040 | tf_op jit(solution)/shard_map/ppermute | solution.py:53
  4.6 5.3 %collective-permute-start.4 = (bf16[8,3584]{1,0:T(8,128)(2,1)S(1)}, bf16[8,3584]{1,0:T(8,128)(2,1)S(1)}, u32[]{:S(2)}, u32[]{:S(2)}) collective-permute-start(bf16[8,3584]{1,0:T(8,128)(2,1)S(1)} %get-tuple-element.21), channel_id=1, source_target_pairs={{0,8},{1,17},{2,10},{3,19},{4,12},{5,21},{6,14},{7,23},{8,0},{9,25... | collective-permute-start | bytes 172040 | tf_op jit(solution)/shard_map/ppermute | solution.py:53
  7.4 5.8 %collective-permute-start.1 = (bf16[16,3584]{1,0:T(8,128)(2,1)S(1)}, bf16[16,3584]{1,0:T(8,128)(2,1)S(1)}, u32[]{:S(2)}, u32[]{:S(2)}) collective-permute-start(bf16[16,3584]{1,0:T(8,128)(2,1)S(1)} %pad_maximum_fusion.6), channel_id=1, source_target_pairs={{0,16},{1,9},{2,18},{3,11},{4,20},{5,13},{6,22},{7,15},{8,24},{9,1... | collective-permute-start | bytes 344072 | tf_op jit(solution)/shard_map/ppermute | solution.py:53
  9.9 6.1 %collective-permute-start.5 = (bf16[16,3584]{1,0:T(8,128)(2,1)S(1)}, bf16[16,3584]{1,0:T(8,128)(2,1)S(1)}, u32[]{:S(2)}, u32[]{:S(2)}) collective-permute-start(bf16[16,3584]{1,0:T(8,128)(2,1)S(1)} %pad_maximum_fusion.7), channel_id=1, source_target_pairs={{0,4},{1,3},{2,6},{3,1},{4,0},{5,7},{6,2},{7,5},{8,12},{9,11},{10,... | collective-permute-start | bytes 344072 | tf_op jit(solution)/shard_map/ppermute | solution.py:53
  13.2 6.1 %collective-permute-start.2 = (bf16[32,3584]{1,0:T(8,128)(2,1)S(1)}, bf16[32,3584]{1,0:T(8,128)(2,1)S(1)}, u32[]{:S(2)}, u32[]{:S(2)}) collective-permute-start(bf16[32,3584]{1,0:T(8,128)(2,1)S(1)} %pad_maximum_fusion.4), channel_id=1, source_target_pairs={{0,2},{1,5},{2,0},{3,7},{4,6},{5,1},{6,4},{7,3},{8,10},{9,13},{10,... | collective-permute-start | bytes 688136 | tf_op jit(solution)/shard_map/ppermute | solution.py:53
  16.0 9.4 %collective-permute-start.6 = (bf16[32,3584]{1,0:T(8,128)(2,1)S(1)}, bf16[32,3584]{1,0:T(8,128)(2,1)S(1)}, u32[]{:S(2)}, u32[]{:S(2)}) collective-permute-start(bf16[32,3584]{1,0:T(8,128)(2,1)S(1)} %pad_maximum_fusion.5), channel_id=1, source_target_pairs={{0,16},{1,9},{2,18},{3,11},{4,20},{5,13},{6,22},{7,15},{8,24},{9,1... | collective-permute-start | bytes 688136 | tf_op jit(solution)/shard_map/ppermute | solution.py:53
  19.3 11.7 %collective-permute-start.3 = (bf16[64,3584]{1,0:T(8,128)(2,1)S(1)}, bf16[64,3584]{1,0:T(8,128)(2,1)S(1)}, u32[]{:S(2)}, u32[]{:S(2)}) collective-permute-start(bf16[64,3584]{1,0:T(8,128)(2,1)S(1)} %pad_maximum_fusion.2), channel_id=1, source_target_pairs={{0,4},{1,3},{2,6},{3,1},{4,0},{5,7},{6,2},{7,5},{8,12},{9,11},{10,... | collective-permute-start | bytes 1376264 | tf_op jit(solution)/shard_map/ppermute | solution.py:53
  25.5 8.5 %collective-permute-start.7 = (bf16[64,3584]{1,0:T(8,128)(2,1)S(1)}, bf16[64,3584]{1,0:T(8,128)(2,1)S(1)}, u32[]{:S(2)}, u32[]{:S(2)}) collective-permute-start(bf16[64,3584]{1,0:T(8,128)(2,1)S(1)} %pad_maximum_fusion.3), channel_id=1, source_target_pairs={{0,2},{1,5},{2,0},{3,7},{4,6},{5,1},{6,4},{7,3},{8,10},{9,13},{10,... | collective-permute-start | bytes 1376264 | tf_op jit(solution)/shard_map/ppermute | solution.py:53
  31.1 4.9 %collective-permute-start.8 = (bf16[128,3584]{1,0:T(8,128)(2,1)S(1)}, bf16[128,3584]{1,0:T(8,128)(2,1)S(1)}, u32[]{:S(2)}, u32[]{:S(2)}) collective-permute-start(bf16[128,3584]{1,0:T(8,128)(2,1)S(1)} %pad_maximum_fusion), channel_id=1, source_target_pairs={{0,1},{1,0},{2,3},{3,2},{4,5},{5,4},{6,7},{7,6},{8,9},{9,8},{10,11... | collective-permute-start | bytes 2752520 | tf_op jit(solution)/shard_map/ppermute | solution.py:57
  40.1 4.6 %collective-permute-start.13 = (f32[3,8,64]{2,1,0:T(8,128)S(1)}, f32[3,8,64]{2,1,0:T(8,128)S(1)}, u32[]{:S(2)}, u32[]{:S(2)}) collective-permute-start(f32[3,8,64]{2,1,0:T(8,128)S(1)} %add_select_fusion.2), channel_id=1, source_target_pairs={{0,6},{1,7},{2,4},{3,5},{4,2},{5,3},{6,0},{7,1},{8,14},{9,15},{10,... | collective-permute-start | bytes 18440 | tf_op jit(solution)/shard_map/ppermute | solution.py:212
  42.6 3.7 %collective-permute-start.12 = (f32[3,8,64]{2,1,0:T(8,128)S(1)}, f32[3,8,64]{2,1,0:T(8,128)S(1)}, u32[]{:S(2)}, u32[]{:S(2)}) collective-permute-start(f32[3,8,64]{2,1,0:T(8,128)S(1)} %add_select_fusion.2), channel_id=1, source_target_pairs={{0,4},{1,5},{2,6},{3,7},{4,0},{5,1},{6,2},{7,3},{8,12},{9,13},{10,... | collective-permute-start | bytes 18440 | tf_op jit(solution)/shard_map/ppermute | solution.py:212
  46.9 5.6 %collective-permute-start.16 = (f32[3,8,64]{2,1,0:T(8,128)S(1)}, f32[3,8,64]{2,1,0:T(8,128)S(1)}, u32[]{:S(2)}, u32[]{:S(2)}) collective-permute-start(f32[3,8,64]{2,1,0:T(8,128)S(1)} %add_select_fusion.1), channel_id=1, source_target_pairs={{0,24},{1,25},{2,26},{3,27},{4,28},{5,29},{6,30},{7,31},{8,16},{9,... | collective-permute-start | bytes 18440 | tf_op jit(solution)/shard_map/ppermute | solution.py:212
  48.4 4.6 %collective-permute-start.15 = (f32[3,8,64]{2,1,0:T(8,128)S(1)}, f32[3,8,64]{2,1,0:T(8,128)S(1)}, u32[]{:S(2)}, u32[]{:S(2)}) collective-permute-start(f32[3,8,64]{2,1,0:T(8,128)S(1)} %add_select_fusion.1), channel_id=1, source_target_pairs={{0,16},{1,17},{2,18},{3,19},{4,20},{5,21},{6,22},{7,23},{8,24},{9,... | collective-permute-start | bytes 18440 | tf_op jit(solution)/shard_map/ppermute | solution.py:212
  48.4 4.7 %collective-permute-start.14 = (f32[3,8,64]{2,1,0:T(8,128)S(1)}, f32[3,8,64]{2,1,0:T(8,128)S(1)}, u32[]{:S(2)}, u32[]{:S(2)}) collective-permute-start(f32[3,8,64]{2,1,0:T(8,128)S(1)} %add_select_fusion.1), channel_id=1, source_target_pairs={{0,8},{1,9},{2,10},{3,11},{4,12},{5,13},{6,14},{7,15},{8,0},{9,1},... | collective-permute-start | bytes 18440 | tf_op jit(solution)/shard_map/ppermute | solution.py:212
  57.1 6.3 %collective-permute-start.22 = (bf16[128,3584]{1,0:T(8,128)(2,1)S(1)}, bf16[128,3584]{1,0:T(8,128)(2,1)S(1)}, u32[]{:S(2)}, u32[]{:S(2)}) collective-permute-start(bf16[128,3584]{1,0:T(8,128)(2,1)S(1)} %get-tuple-element.20), channel_id=1, source_target_pairs={{0,1},{1,0},{2,3},{3,2},{4,5},{5,4},{6,7},{7,6},{8,9},{9,8},{10,11... | collective-permute-start | bytes 2752520 | tf_op jit(solution)/shard_map/ppermute | solution.py:57
  58.1 6.7 %collective-permute-start.17 = (bf16[128,3584]{1,0:T(8,128)(2,1)S(1)}, bf16[128,3584]{1,0:T(8,128)(2,1)S(1)}, u32[]{:S(2)}, u32[]{:S(2)}) collective-permute-start(bf16[128,3584]{1,0:T(8,128)(2,1)S(1)} %get-tuple-element.19), channel_id=1, source_target_pairs={{0,1},{1,0},{2,3},{3,2},{4,5},{5,4},{6,7},{7,6},{8,9},{9,8},{10,11... | collective-permute-start | bytes 2752520 | tf_op jit(solution)/shard_map/ppermute | solution.py:57
  63.6 13.0 %collective-permute-start.23 = (bf16[64,3584]{1,0:T(8,128)(2,1)S(1)}, bf16[64,3584]{1,0:T(8,128)(2,1)S(1)}, u32[]{:S(2)}, u32[]{:S(2)}) collective-permute-start(bf16[64,3584]{1,0:T(8,128)(2,1)S(1)} %slice.99), channel_id=1, source_target_pairs={{0,2},{1,5},{2,0},{3,7},{4,6},{5,1},{6,4},{7,3},{8,10},{9,13},{10,... | collective-permute-start | bytes 1376264 | tf_op jit(solution)/shard_map/ppermute | solution.py:53
  65.0 13.7 %collective-permute-start.18 = (bf16[64,3584]{1,0:T(8,128)(2,1)S(1)}, bf16[64,3584]{1,0:T(8,128)(2,1)S(1)}, u32[]{:S(2)}, u32[]{:S(2)}) collective-permute-start(bf16[64,3584]{1,0:T(8,128)(2,1)S(1)} %slice.91), channel_id=1, source_target_pairs={{0,4},{1,3},{2,6},{3,1},{4,0},{5,7},{6,2},{7,5},{8,12},{9,11},{10,... | collective-permute-start | bytes 1376264 | tf_op jit(solution)/shard_map/ppermute | solution.py:53
  76.7 9.5 %collective-permute-start.24 = (bf16[32,3584]{1,0:T(8,128)(2,1)S(1)}, bf16[32,3584]{1,0:T(8,128)(2,1)S(1)}, u32[]{:S(2)}, u32[]{:S(2)}) collective-permute-start(bf16[32,3584]{1,0:T(8,128)(2,1)S(1)} %slice.101), channel_id=1, source_target_pairs={{0,16},{1,9},{2,18},{3,11},{4,20},{5,13},{6,22},{7,15},{8,24},{9,1... | collective-permute-start | bytes 688136 | tf_op jit(solution)/shard_map/ppermute | solution.py:53
  78.8 9.1 %collective-permute-start.19 = (bf16[32,3584]{1,0:T(8,128)(2,1)S(1)}, bf16[32,3584]{1,0:T(8,128)(2,1)S(1)}, u32[]{:S(2)}, u32[]{:S(2)}) collective-permute-start(bf16[32,3584]{1,0:T(8,128)(2,1)S(1)} %slice.93), channel_id=1, source_target_pairs={{0,2},{1,5},{2,0},{3,7},{4,6},{5,1},{6,4},{7,3},{8,10},{9,13},{10,... | collective-permute-start | bytes 688136 | tf_op jit(solution)/shard_map/ppermute | solution.py:53
  86.3 4.9 %collective-permute-start.25 = (bf16[16,3584]{1,0:T(8,128)(2,1)S(1)}, bf16[16,3584]{1,0:T(8,128)(2,1)S(1)}, u32[]{:S(2)}, u32[]{:S(2)}) collective-permute-start(bf16[16,3584]{1,0:T(8,128)(2,1)S(1)} %slice.103), channel_id=1, source_target_pairs={{0,4},{1,3},{2,6},{3,1},{4,0},{5,7},{6,2},{7,5},{8,12},{9,11},{10,... | collective-permute-start | bytes 344072 | tf_op jit(solution)/shard_map/ppermute | solution.py:53
  88.0 6.5 %collective-permute-start.20 = (bf16[16,3584]{1,0:T(8,128)(2,1)S(1)}, bf16[16,3584]{1,0:T(8,128)(2,1)S(1)}, u32[]{:S(2)}, u32[]{:S(2)}) collective-permute-start(bf16[16,3584]{1,0:T(8,128)(2,1)S(1)} %slice.95), channel_id=1, source_target_pairs={{0,16},{1,9},{2,18},{3,11},{4,20},{5,13},{6,22},{7,15},{8,24},{9,1... | collective-permute-start | bytes 344072 | tf_op jit(solution)/shard_map/ppermute | solution.py:53
  91.2 4.2 %collective-permute-start.26 = (bf16[8,3584]{1,0:T(8,128)(2,1)S(1)}, bf16[8,3584]{1,0:T(8,128)(2,1)S(1)}, u32[]{:S(2)}, u32[]{:S(2)}) collective-permute-start(bf16[8,3584]{1,0:T(8,128)(2,1)S(1)} %slice.105), channel_id=1, source_target_pairs={{0,8},{1,17},{2,10},{3,19},{4,12},{5,21},{6,14},{7,23},{8,0},{9,25... | collective-permute-start | bytes 172040 | tf_op jit(solution)/shard_map/ppermute | solution.py:53
  94.5 4.2 %collective-permute-start.21 = (bf16[8,3584]{1,0:T(8,128)(2,1)S(1)}, bf16[8,3584]{1,0:T(8,128)(2,1)S(1)}, u32[]{:S(2)}, u32[]{:S(2)}) collective-permute-start(bf16[8,3584]{1,0:T(8,128)(2,1)S(1)} %slice.97), channel_id=1, source_target_pairs={{0,8},{1,17},{2,10},{3,19},{4,12},{5,21},{6,14},{7,23},{8,0},{9,25... | collective-permute-start | bytes 172040 | tf_op jit(solution)/shard_map/ppermute | solution.py:53
  (5 other events, 38.5 us)
